TPU v7x, 128 devices: a whole 4x4x4 slice. The times are simulated.
128 devices in a mesh: section: 2 (over core), dev: 64 (over x, z, y).
Axes of the slice: x: 4, y: 4, z: 4, core: 2. Of those that a mesh axis runs over, the one named last changes fastest.
Arguments:
- indices: int32 [8192, 32, 8], P(('section', 'dev')), may hold values from 0 to 131071
- pool_len: int32 [32], replicated, may hold values from 1 to 8
- tables: bfloat16 [4194304, 128], P(('section', 'dev')), may hold values from -3 to 3
- w_first: bfloat16 [4096, 4096], P('dev', 'section'), may hold values from -0.09375 to 0.09375
- b_first: bfloat16 [4096], P('section'), may hold values from -3 to 3
- w_out: bfloat16 [4096], P('section'), may hold values from -0.09375 to 0.09375
Outputs:
- logits: float32 [8192], P('dev')
Inputs may be any that keep to these rules, and one draw needn't show every extreme that they name: `indices`: ids of rows of the table named by the second index.
All inputs are finite; a program needn't handle non-finite values.
Results may differ from a plain program's by a relative error of at most 0.0095.
Values may be sent and summed in bfloat16 or wider, within the bound.
A program may use at most 128 MiB of HBM per device.

v0:
```python
import jax
import jax.numpy as jnp
from jax import lax
from jax.sharding import PartitionSpec as P


def sent_to_all(shard, axis):
    devices = lax.axis_size(axis)
    return lax.all_to_all(
        jnp.broadcast_to(shard[None], (devices, *shard.shape)), axis, 0, 0, tiled=True
    )


def in_order(tiles, dim):
    shape = list(tiles.shape[1:])
    shape[dim] *= tiles.shape[0]
    return jnp.moveaxis(tiles, 0, dim).reshape(shape)


def collect(shard, axis, dim):
    tiles = sent_to_all(shard, axis)
    return in_order(tiles, dim)


def gathered_total(shard, axis):
    return lax.all_gather(shard, axis).sum(0)


def body(indices, pool_len, tables, w_first, b_first, w_out):
    sec_count = lax.axis_size("section")
    dev_count = lax.axis_size("dev")
    devices = sec_count * dev_count
    dev_rows, n_tables, pool_size = indices.shape
    rows_dev, emb_width = tables.shape
    row_split = devices // n_tables
    position = lax.axis_index("section") * dev_count + lax.axis_index("dev")
    table_id = position // row_split
    first_row = position % row_split * rows_dev
    outgoing = jnp.repeat(indices, row_split, axis=1)
    arrived = lax.all_to_all(outgoing, ("section", "dev"), split_axis=1, concat_axis=0, tiled=True)
    all_rows = devices * dev_rows
    wanted = arrived.reshape(all_rows, pool_size) - first_row
    live_slots = jnp.sum(jnp.where(jnp.arange(n_tables) == table_id, pool_len, 0))
    usable = (wanted >= 0) & (wanted < rows_dev) & (jnp.arange(pool_size)[None, :] < live_slots)
    safe_rows = jnp.where(usable, wanted, 0)
    looked = jnp.take(tables, safe_rows, axis=0)
    picked = jnp.where(usable[:, :, None], looked, jnp.zeros((), jnp.bfloat16))
    partial_value = jnp.sum(picked.astype(jnp.float32), axis=1).astype(jnp.bfloat16)
    ordered = jnp.transpose(
        partial_value.reshape(dev_count, sec_count, dev_rows, emb_width), (1, 0, 2, 3)
    )
    received = lax.all_to_all(
        ordered.reshape(devices, dev_rows, emb_width),
        ("section", "dev"),
        split_axis=0,
        concat_axis=0,
        tiled=True,
    )
    summed = jnp.sum(
        received.reshape(n_tables, row_split, dev_rows, emb_width).astype(jnp.float32), axis=1
    )
    features = jnp.transpose(summed.astype(jnp.bfloat16), (1, 0, 2)).reshape(
        dev_rows, n_tables * emb_width
    )
    samples = collect(features, "section", 0)
    whole_weights = lax.all_gather(w_first, "dev", axis=0, tiled=True)
    pre_act = jnp.dot(samples, whole_weights, preferred_element_type=jnp.float32)
    hidden = jnp.maximum(pre_act + b_first.astype(jnp.float32)[None, :], 0.0)
    logit_part = jnp.sum(hidden * w_out.astype(jnp.float32)[None, :], axis=1)
    return gathered_total(logit_part, "section")


def solution(mesh):
    placed = (
        P(("section", "dev"), None, None),
        P(),
        P(("section", "dev"), None),
        P("dev", "section"),
        P("section"),
        P("section"),
    )
    return jax.shard_map(body, mesh=mesh, in_specs=placed, out_specs=P("dev"), check_vma=False)
```

profile of v0, /device:TPU:1, one launch (start us, length us, event | category | flops | bytes accessed | tf_op | source)
XLA Modules:
  0.0 371.7 jit_solution(8074114564195128807)
XLA Ops:
  6.5 0.0 all-gather.4.cloned.1.call-start
  6.5 0.7 all-gather.4.cloned.1.call-update
  7.3 0.9 broadcast_in_dim.42
  8.2 1.0 reshape.131
  9.2 11.5 %all-to-all-start = ((s32[128,1,512]{2,1,0:T(1,128)}), s32[128,1,512]{2,1,0:T(1,128)S(1)}, u32[]{:S(2)}, u32[]{:S(2)}) async-start(s32[128,1,512]{2,1,0:T(1,128)} %reshape.131), calls=%async_computation | async-start | bytes 524288 | tf_op jit(solution)/shard_map/all_to_all | solution.py:40
  20.7 1.3 fusion.5
  22.0 0.6 iota_compare_fusion
  22.7 8.8 %all-to-all-done = s32[128,1,512]{2,1,0:T(1,128)S(1)} async-done(((s32[128,1,512]{2,1,0:T(1,128)}), s32[128,1,512]{2,1,0:T(1,128)S(1)}, u32[]{:S(2)}, u32[]{:S(2)}) %all-to-all-start) | async-done | bytes 262176 | tf_op jit(solution)/shard_map/all_to_all | solution.py:40
  31.5 0.5 broadcast.117
  32.0 1.3 reduce.3
  33.3 0.1 reshape.132
  33.5 0.1 copy.13
  33.6 0.2 sub.42
  33.8 0.2 sub.40
  33.9 0.1 compare_select_fusion
  34.1 2.6 copy.17
  36.6 3.6 reshape.120
  40.3 0.2 and_and_fusion
  40.5 1.7 copy.14
  42.2 1.7 copy.15
  43.9 222.3 %gather_fusion = bf16[65536,128]{1,0:T(8,128)(2,1)} fusion(bf16[32768,128]{1,0:T(8,128)(2,1)} %param.8, s32[65536]{0:T(1024)S(1)} %broadcast_clamp_fusion), kind=kCustom, calls=%fused_computation | custom fusion | bytes 33816576 | tf_op jit(solution)/shard_map/jit(_take)/gather | solution.py:46
  266.2 0.0 copy-start
  266.2 0.0 copy-start.1
  266.2 46.4 %fusion.1 = bf16[8192,128]{1,0:T(8,128)(2,1)S(1)} fusion(bf16[65536,128]{1,0:T(8,128)(2,1)} %gather_fusion, pred[8192,8]{1,0:T(8,128)(4,1)S(1)} %copy.15, pred[8192,8]{1,0:T(8,128)(4,1)S(1)} %copy.14), kind=kLoop, calls=%fused_computation.3 | loop fusion | flops 24117248 | bytes 19005440 | tf_op jit(solution)/shard_map/reduce_sum | solution.py:48
  312.6 1.5 copy.18
  314.1 4.3 %all-to-all-start.1 = ((bf16[128,64,128]{2,1,0:T(8,128)(2,1)}), bf16[128,64,128]{2,1,0:T(8,128)(2,1)S(1)}, u32[]{:S(2)}, u32[]{:S(2)}) async-start(bf16[128,64,128]{2,1,0:T(8,128)(2,1)} %bitcast.41), calls=%async_computation.1 | async-start | bytes 4194304 | tf_op jit(solution)/shard_map/all_to_all | solution.py:52
  318.5 0.0 copy-done
  318.5 0.0 copy-done.1
  318.5 30.1 %all-to-all-done.1 = bf16[128,64,128]{2,1,0:T(8,128)(2,1)S(1)} async-done(((bf16[128,64,128]{2,1,0:T(8,128)(2,1)}), bf16[128,64,128]{2,1,0:T(8,128)(2,1)S(1)}, u32[]{:S(2)}, u32[]{:S(2)}) %all-to-all-start.1) | async-done | bytes 2097184 | tf_op jit(solution)/shard_map/all_to_all | solution.py:52
  348.6 0.4 bitcast_reduce_fusion
  348.9 0.1 copy_bitcast_fusion
  349.0 0.1 broadcast_in_dim.49
  349.1 5.1 %all_to_all.19 = bf16[2,64,4096]{2,1,0:T(8,128)(2,1)S(1)} all-to-all(bf16[2,64,4096]{2,1,0:T(8,128)(2,1)S(1)} %broadcast_in_dim.49), channel_id=1, replica_groups=mesh['section'=2,'dev'=64] {'section'}, dimensions={0} | all-to-all | bytes 2097152 | tf_op jit(solution)/shard_map/all_to_all | solution.py:9
  354.2 0.0 all-gather.4.cloned.1.call-done
  354.3 8.2 %fusion.4 = f32[128]{0:T(128)S(1)} fusion(bf16[128,4096]{1,0:T(8,128)(2,1)S(1)} %bitcast.42, bf16[4096,2048]{1,0:T(8,128)(2,1)} %all-gather.4.cloned.1.call-done, f32[2048]{0:T(1024)S(1)} %convert_element_type.5, f32[2048]{0:T(1024)S(1)} %convert_element_type.4), kind=kOutput, calls=%fused_computation.8 | convolution fusion | flops 2148532224 | bytes 17842688 | tf_op jit(solution)/shard_map/dot_general | solution.py:67
  362.5 1.8 all-gather.1
  364.3 0.5 reduce_sum.55
  (4 shorter events, 0.1 us)
Async XLA Ops:
  6.5 347.7 %all-gather.4.cloned.1.call-start = ((), (), s32[]{:S(2)}) async-start(), calls=%async_computation.3 | async-start | bytes 17039360 | tf_op jit(solution)/shard_map/all_gather | solution.py:66
  9.2 22.3 %all-to-all-start = ((s32[128,1,512]{2,1,0:T(1,128)}), s32[128,1,512]{2,1,0:T(1,128)S(1)}, u32[]{:S(2)}, u32[]{:S(2)}) async-start(s32[128,1,512]{2,1,0:T(1,128)} %reshape.131), calls=%async_computation | async-start | bytes 524288 | tf_op jit(solution)/shard_map/all_to_all | solution.py:40
  266.2 52.3 %copy-start = (bf16[2048]{0:T(1024)(128)(2,1)S(1)}, bf16[2048]{0:T(1024)(128)(2,1)}, u32[]{:S(2)}) copy-start(bf16[2048]{0:T(1024)(128)(2,1)} %param.10) | copy-start | bytes 12292
  266.2 52.3 %copy-start.1 = (bf16[2048]{0:T(1024)(128)(2,1)S(1)}, bf16[2048]{0:T(1024)(128)(2,1)}, u32[]{:S(2)}) copy-start(bf16[2048]{0:T(1024)(128)(2,1)} %param.11) | copy-start | bytes 12292
  314.1 34.4 %all-to-all-start.1 = ((bf16[128,64,128]{2,1,0:T(8,128)(2,1)}), bf16[128,64,128]{2,1,0:T(8,128)(2,1)S(1)}, u32[]{:S(2)}, u32[]{:S(2)}) async-start(bf16[128,64,128]{2,1,0:T(8,128)(2,1)} %bitcast.41), calls=%async_computation.1 | async-start | bytes 4194304 | tf_op jit(solution)/shard_map/all_to_all | solution.py:52
Sparse Core Ops, SparseCore 0:
  10.2 107.0 all-gather.3
where the time goes:
time: 372 us
  local copies, waits for them, and re-layouts  237 us (64%)
  other arithmetic  50.9 us (14%)
  waiting for transfers between devices  39.6 us (11%)
  starting transfers between devices  15.8 us (4%)
  between operations  13.6 us (4%)
  matrix products  8.24 us (2%)
  blocking collectives  6.93 us (2%)
    gather x1, local copies, waits for them, and re-layouts, body(): looked = jnp.take(tables, safe_rows, axis=0)  222 us
    reduce_sum x1, other arithmetic, body(): jnp.sum(picked.astype(jnp.float32), axis=1).astype(jnp.bfloat16)  46.4 us
    all_to_all x1, waiting for transfers between devices, body(): lax.all_to_all(ordered.reshape(devices, dev_rows, emb_width), ('section',...  30.1 us
    all_to_all x1, starting transfers between devices, body(): lax.all_to_all(outgoing, ('section', 'dev'), split_axis=1, concat_axis=0,...  11.5 us
    all_to_all x1, waiting for transfers between devices, body(): lax.all_to_all(outgoing, ('section', 'dev'), split_axis=1, concat_axis=0,...  8.81 us
    dot_general x1, matrix products, body(): jnp.dot(samples, whole_weights, preferred_element_type=jnp.float32)  8.24 us
  transfers between devices with their start and end apart: 3, of which 2 were waited for; matrix products, arithmetic and copies ran while one was open for 77% of the time, Pallas kernels for 0%

commit v1 on v0

v1 whole, which is shorter than its diff:
```python
import functools

import jax
import jax.numpy as jnp
from jax import lax
from jax.experimental import pallas as pl
from jax.experimental.pallas import tpu as pltpu
from jax.sharding import Mesh, PartitionSpec as P

TABLES = 32
SRC, BAGS, CAP = 128, 64, 512
CUTS = ((64, 32, 32), (16, 16, 16, 16, 32, 32), (32,) * 4)
G = 8
TB = 2048
NBUF = 4

def lookup_kernel(keys, table, out, rows_v, rows_s, tab, stage, buf, sem_s, sem_t):
    nb = table.shape[0] // TB
    def fetch(i, slot):
        return pltpu.make_async_copy(table.at[pl.ds(i * TB, TB), :], stage.at[slot], sem_t.at[slot])
    for i in range(NBUF):
        fetch(i, i).start()
    k = keys[...]
    n = jnp.sum((k < (BAGS << 15)).astype(jnp.int32), axis=1, keepdims=True)
    for r in range(4):
        rows_v[r * SRC:(r + 1) * SRC, :] = k[:, r * 128:(r + 1) * 128] & 32767
    rows_v[4 * SRC:, :] = jnp.broadcast_to(n, (SRC, 128))
    cps = [pltpu.make_async_copy(rows_v.at[pl.ds(i * SRC, SRC), :], rows_s.at[pl.ds(i * SRC, SRC), :], sem_s.at[i]) for i in range(5)]
    cps[4].start()
    cps[0].start()
    cps[1].start()
    buf[...] = jnp.zeros_like(buf)

    @pl.loop(0, nb // NBUF)
    def _(h):
        for slot in range(NBUF):
            i = h * NBUF + slot
            fetch(i, slot).wait()
            base = pl.multiple_of(i * TB, TB)
            tab[pl.ds(base, TB), :] = stage[slot].astype(jnp.float32)
            @pl.when(i + NBUF < nb)
            def _():
                fetch(i + NBUF, slot).start()

    cps[4].wait()
    cps[0].wait()
    cps[1].wait()
    most = lax.fori_loop(0, SRC, lambda c, m: jnp.maximum(m, rows_s[4 * SRC + c, 0]), 0, unroll=False)
    @pl.when(most > 256)
    def _():
        cps[2].start()
        cps[3].start()
        cps[2].wait()
        cps[3].wait()
    bag_row = lax.broadcasted_iota(jnp.int32, (BAGS, 256), 0)

    @pl.loop(0, SRC // G)
    def _(grp):
        @pl.loop(0, G)
        def _(g):
            c = grp * G + g
            n = rows_s[4 * SRC + c, 0]
            for r in range(4):
                def some(r=r):
                    view = rows_s.at[r * SRC + c]
                    at = 0
                    for size in CUTS[min(r, 2)]:
                        def block(at=at, size=size):
                            for u in range(at, at + size):
                                buf[g, r * 128 + u: r * 128 + u + 1, :] = tab[pl.ds(view[u], 1), :]
                        if at == 0:
                            block()
                        else:
                            pl.when(n > r * 128 + at)(block)
                        at += size
                if r == 0:
                    some()
                else:
                    pl.when(n > r * 128)(some)
        def part(g, lo):
            kk = keys[pl.ds(grp * G + g, 1), lo:lo + 256] >> 15
            oh = jnp.where(kk == bag_row, 1.0, 0.0).astype(jnp.bfloat16)
            return jnp.dot(oh, buf[g, lo:lo + 256, :].astype(jnp.bfloat16), preferred_element_type=jnp.float32)
        most = rows_s[4 * SRC + grp * G, 0]
        for g in range(1, G):
            most = jnp.maximum(most, rows_s[4 * SRC + grp * G + g, 0])
        for g in range(G):
            out[grp * G + g] = part(g, 0).astype(jnp.bfloat16)
        @pl.when(most > 256)
        def _():
            for g in range(G):
                out[grp * G + g] = (part(g, 0) + part(g, 256)).astype(jnp.bfloat16)


def lookup(keys, table):
    return pl.pallas_call(
        lookup_kernel,
        out_shape=jax.ShapeDtypeStruct((SRC, BAGS, 128), jnp.bfloat16),
        in_specs=[pl.BlockSpec(memory_space=pltpu.VMEM), pl.BlockSpec(memory_space=pl.ANY)],
        out_specs=pl.BlockSpec(memory_space=pltpu.VMEM),
        scratch_shapes=[
            pltpu.VMEM((SRC * 5, 128), jnp.int32),
            pltpu.SMEM((SRC * 5, 128), jnp.int32),
            pltpu.VMEM((table.shape[0], 128), jnp.float32),
            pltpu.VMEM((NBUF, TB, 128), jnp.bfloat16),
            pltpu.VMEM((G, CAP, 128), jnp.float32),
            pltpu.SemaphoreType.DMA((5,)),
            pltpu.SemaphoreType.DMA((NBUF,)),
        ],
        compiler_params=pltpu.CompilerParams(vmem_limit_bytes=48 << 20),
        cost_estimate=pl.CostEstimate(flops=10**10, bytes_accessed=10**7, transcendentals=0),
    )(keys, table)


LANES = 128
BLKS = CAP // LANES

def bitonic(xs, lane):
    pos = [lane + b * LANES for b in range(BLKS)]
    k = 2
    while k <= CAP:
        d = k // 2
        while d >= 1:
            if d >= LANES:
                step = d // LANES
                new = list(xs)
                for b in range(BLKS):
                    if b & step:
                        continue
                    lo, hi = jnp.minimum(xs[b], xs[b + step]), jnp.maximum(xs[b], xs[b + step])
                    up = ((b * LANES) & k) == 0
                    new[b], new[b + step] = (lo, hi) if up else (hi, lo)
                xs = new
            else:
                low = (lane & d) == 0
                new = []
                for b in range(BLKS):
                    x = xs[b]
                    other = jnp.where(low, pltpu.roll(x, LANES - d, 1), pltpu.roll(x, d, 1))
                    if k >= LANES:
                        up = ((b * LANES) & k) == 0
                        want_min = low if up else jnp.logical_not(low)
                    else:
                        want_min = ((pos[b] & k) == 0) == low
                    new.append(jnp.where(want_min, jnp.minimum(x, other), jnp.maximum(x, other)))
                xs = new
            d //= 2
        k *= 2
    return xs

def rotate_left(xs, lane, amount):
    s = 1
    while s < CAP:
        take = (amount & s) != 0
        if s >= LANES:
            step = s // LANES
            moved = [xs[(b + step) % BLKS] for b in range(BLKS)]
        else:
            rolled = [pltpu.roll(x, LANES - s, 1) for x in xs]
            moved = [jnp.where(lane < LANES - s, rolled[b], rolled[(b + 1) % BLKS]) for b in range(BLKS)]
        xs = [jnp.where(take, m, x) for m, x in zip(moved, xs)]
        s *= 2
    return xs

def prep_kernel(keys, out):
    lane = lax.broadcasted_iota(jnp.int32, (TABLES, LANES), 1)
    xs = bitonic([keys[:, b * LANES:(b + 1) * LANES] for b in range(BLKS)], lane)
    for j in range(4):
        ys = xs
        if j:
            start = sum(jnp.sum((x < (j << 21)).astype(jnp.int32), axis=1, keepdims=True) for x in xs)
            ys = rotate_left(xs, lane, jnp.broadcast_to(start, (TABLES, LANES)))
        for b in range(BLKS):
            mine = (ys[b] >> 21) == j
            out[j, :, b * LANES:(b + 1) * LANES] = jnp.where(mine, ys[b] & ((1 << 21) - 1), 64 << 15)


def prep(keys):
    return pl.pallas_call(
        prep_kernel,
        out_shape=jax.ShapeDtypeStruct((4, TABLES, CAP), jnp.int32),
        in_specs=[pl.BlockSpec(memory_space=pltpu.VMEM)],
        out_specs=pl.BlockSpec(memory_space=pltpu.VMEM),
    )(keys)


def make_keys(indices, pool_len):
    n, t, p = indices.shape
    bag = lax.broadcasted_iota(jnp.int32, (t, p, n), 2)
    slot = lax.broadcasted_iota(jnp.int32, (t, p, n), 1)
    idx = jnp.transpose(indices, (1, 2, 0))
    key = ((idx >> 15) << 21) | (bag << 15) | (idx & 32767)
    key = jnp.where(slot < pool_len[:, None, None], key, 4 << 21)
    return key.reshape(t, p * n)


ALL = ("section", "x", "z", "y")


def body(indices, pool_len, tables, w_first, b_first, w_out):
    x = lax.axis_index("x")
    z = lax.axis_index("z")
    y = lax.axis_index("y")
    quarter = w_first.shape[1] // 4
    w_part = lax.all_to_all(w_first, "x", split_axis=1, concat_axis=0, tiled=True)
    w_all = lax.all_gather(w_part.reshape(4, 64, quarter), ("z", "y"), axis=1)
    w_all = w_all.reshape(-1, quarter)
    bias = lax.dynamic_slice(b_first, (x * quarter,), (quarter,)).astype(jnp.float32)
    scale = lax.dynamic_slice(w_out, (x * quarter,), (quarter,)).astype(jnp.float32)

    lists = prep(make_keys(indices, pool_len))
    lists = jnp.transpose(lists, (1, 0, 2)).reshape(128, CAP)
    keys = lax.all_to_all(lists, ALL, split_axis=0, concat_axis=0, tiled=True)
    partial = lookup(keys, tables)
    ordered = jnp.transpose(partial.reshape(64, 2, BAGS, 128), (1, 0, 2, 3)).reshape(SRC, BAGS, 128)
    received = lax.all_to_all(ordered, ALL, split_axis=0, concat_axis=0, tiled=True)
    pooled = jnp.sum(received.reshape(TABLES, 4, BAGS, 128).astype(jnp.float32), axis=1)
    features = jnp.transpose(pooled.astype(jnp.bfloat16), (1, 0, 2)).reshape(BAGS, TABLES * 128)
    samples = lax.all_gather(features, ("x", "section"), axis=0, tiled=True)
    pre_act = jnp.dot(samples, w_all, preferred_element_type=jnp.float32)
    hidden = jnp.maximum(pre_act + bias[None, :], 0.0)
    logit_part = jnp.sum(hidden * scale[None, :], axis=1)
    parts = lax.all_gather(logit_part, ("section", "x"))
    total = jnp.sum(parts, axis=0)
    return lax.dynamic_slice(total, (x * 128,), (128,))


def solution(mesh):
    grid = Mesh(mesh.devices.reshape(2, 4, 4, 4), ALL)
    dev = ("x", "z", "y")
    placed = (
        P(ALL, None, None),
        P(),
        P(ALL, None),
        P(dev, "section"),
        P("section"),
        P("section"),
    )
    return jax.shard_map(body, mesh=grid, in_specs=placed, out_specs=P(dev), check_vma=False)
```

time: 372 us -> 176 us (0.47)
  local copies, waits for them, and re-layouts: 237 us -> 10.7 us
  blocking collectives: 6.93 us -> 86.8 us
  other arithmetic: 50.9 us -> 2.2 us
  Pallas kernels: 0 us -> 32 us
  starting transfers between devices: 15.8 us -> 0.04 us
  waiting for transfers between devices: 39.6 us -> 24.4 us
    gather x1 -> x0, local copies, waits for them, and re-layouts: 222 us -> none  [body(): looked = jnp.take(tables, safe_rows, axis=0)]
    all_to_all x1 -> x3, blocking collectives: 5.13 us -> 67 us  [the longest x1 36 us: body(): lax.all_to_all(ordered, ALL, split_axis=0, concat_axis=0, tiled=True)]
    reduce_sum x4 -> x2, other arithmetic: 48.6 us -> 0.41 us  [the longest x1 0.38 us: body(): jnp.sum(received.reshape(TABLES, 4, BAGS, 128).astype(jnp.float32), axis=1)]
    all_to_all x2 -> x0, waiting for transfers between devices: 38.9 us -> none  [the longest x1 30.1 us: body(): lax.all_to_all(ordered.reshape(devices, dev_rows, emb_width), ('section',...]
    pallas_call x0 -> x2, Pallas kernels: none -> 32 us  [the longest x1 26.7 us: lookup(): pl.pallas_call(lookup_kernel, out_shape=jax.ShapeDtypeStruct((SRC, BAGS,...]
    all_gather x1 -> x2, waiting for transfers between devices: 0.01 us -> 24.4 us  [the longest x1 24.4 us: body(): samples = lax.all_gather(features, ('x', 'section'), axis=0, tiled=True)]
    all_gather x1, blocking collectives: 1.81 us -> 19.8 us  [body(): parts = lax.all_gather(logit_part, ('section', 'x'))]
    all_to_all x2 -> x0, starting transfers between devices: 15.8 us -> none  [the longest x1 11.5 us: body(): lax.all_to_all(outgoing, ('section', 'dev'), split_axis=1, concat_axis=0,...]
  transfers between devices with their start and end apart: 3 -> 2, of which waited for: 2 -> 1; matrix products, arithmetic and copies ran while one was open for 77% -> 6% of each run, Pallas kernels for 0% -> 18%
where the time goes in v1:
time: 176 us
  blocking collectives  86.8 us (49%)
  Pallas kernels  32 us (18%)
  waiting for transfers between devices  24.4 us (14%)
  between operations  13.5 us (8%)
  local copies, waits for them, and re-layouts  10.7 us (6%)
  matrix products  5.86 us (3%)
  other arithmetic  2.2 us (1%)
    all_to_all x1, blocking collectives, body(): lax.all_to_all(ordered, ALL, split_axis=0, concat_axis=0, tiled=True)  36 us
    pallas_call x1, Pallas kernels, lookup(): pl.pallas_call(lookup_kernel, out_shape=jax.ShapeDtypeStruct((SRC, BAGS,...  26.7 us
    all_gather x1, waiting for transfers between devices, body(): samples = lax.all_gather(features, ('x', 'section'), axis=0, tiled=True)  24.4 us
    all_to_all x1, blocking collectives, body(): keys = lax.all_to_all(lists, ALL, split_axis=0, concat_axis=0, tiled=True)  20.8 us
    all_gather x1, blocking collectives, body(): parts = lax.all_gather(logit_part, ('section', 'x'))  19.8 us
    all_to_all x1, blocking collectives, body(): lax.all_to_all(w_first, 'x', split_axis=1, concat_axis=0, tiled=True)  10.2 us
    dot_general x1, matrix products, body(): pre_act = jnp.dot(samples, w_all, preferred_element_type=jnp.float32)  5.86 us
    pallas_call x1, Pallas kernels, prep(): pl.pallas_call(prep_kernel, out_shape=jax.ShapeDtypeStruct((4, TABLES, CA...  5.34 us
  transfers between devices with their start and end apart: 2, of which 1 were waited for; matrix products, arithmetic and copies ran while one was open for 6% of the time, Pallas kernels for 18%

profile of v1, /device:TPU:1, one launch (start us, length us, event | category | flops | bytes accessed | tf_op | source)
XLA Modules:
  0.0 175.5 jit_solution(13325025003927872243)
XLA Ops:
  6.5 0.0 all-gather.8.cloned.1.call-start
  6.5 1.0 copy.31
  7.5 10.2 %all_to_all.33 = bf16[64,4,512]{2,0,1:T(8,128)(2,1)S(1)} all-to-all(bf16[64,4,512]{2,0,1:T(8,128)(2,1)S(1)} %bitcast.33), channel_id=1, replica_groups=mesh['section'=2,'x'=4,'z'=4,'y'=4] {'x'}, dimensions={1} | all-to-all | bytes 524288 | tf_op jit(solution)/shard_map/all_to_all | solution.py:205
  17.7 0.9 copy.23
  18.6 0.0 all-gather.8.cloned.1.call-update
  18.6 0.0 all-gather.6.cloned.1.call-start
  18.7 1.0 bitcast_select_fusion
  19.7 0.7 reshape.29.keys
  20.4 5.3 %shard_map.64 = s32[4,32,512]{2,1,0:T(8,128)} custom-call(s32[32,512]{1,0:T(8,128)} %reshape.29.keys), custom_call_target="tpu_custom_call" | custom-call | tf_op jit(solution)/shard_map/pallas_call | solution.py:179
  25.8 1.1 copy.18
  26.9 0.4 all_to_all.29
  27.2 20.8 %all_to_all.34 = s32[128,1,512]{2,1,0:T(1,128)S(1)} all-to-all(s32[128,1,512]{2,1,0:T(1,128)S(1)} %all_to_all.29), channel_id=1, replica_groups=mesh['section'=2,'x'=4,'z'=4,'y'=4] {'section','x','z','y'}, dimensions={0} | all-to-all | bytes 524288 | tf_op jit(solution)/shard_map/all_to_all | solution.py:213
  48.1 26.7 %shard_map.65 = bf16[128,64,128]{2,1,0:T(8,128)(2,1)S(1)} custom-call(s32[128,512]{1,0:T(8,128)S(1)} %bitcast.28, bf16[32768,128]{1,0:T(8,128)(2,1)} %table.1), custom_call_target="tpu_custom_call" | custom-call | flops 10000000000 | bytes 10000000 | tf_op jit(solution)/shard_map/pallas_call | solution.py:96
  74.8 0.2 copy.20
  74.9 36.0 %all_to_all.35 = bf16[128,64,128]{2,1,0:T(8,128)(2,1)S(1)} all-to-all(bf16[128,64,128]{2,1,0:T(8,128)(2,1)S(1)} %bitcast.29), channel_id=1, replica_groups=mesh['section'=2,'x'=4,'z'=4,'y'=4] {'section','x','z','y'}, dimensions={0} | all-to-all | bytes 4194304 | tf_op jit(solution)/shard_map/all_to_all | solution.py:216
  111.0 0.4 bitcast_reduce_fusion
  111.3 0.9 copy_bitcast_fusion
  112.2 0.0 all-gather.6.cloned.1.call-update
  112.3 0.8 dynamic-slice_convert_fusion
  113.0 0.0 all-gather.8.cloned.1.call-done
  113.0 5.0 %copy.24 = bf16[4,1024,512]{2,1,0:T(8,128)(2,1)} copy(bf16[4,1024,512]{2,0,1:T(4,128)(2,1)} %all-gather.8.cloned.1.call-done) | data formatting | bytes 8388608 | tf_op jit(solution)/shard_map/all_gather | solution.py:206
  118.0 24.4 %all-gather.6.cloned.1.call-done = bf16[512,4096]{1,0:T(8,128)(2,1)} async-done(((bf16[64,4096]{1,0:T(8,128)(2,1)}), bf16[512,4096]{1,0:T(8,128)(2,1)}) %all-gather.6.cloned.1.call-update) | async-done | bytes 4194320 | tf_op jit(solution)/shard_map/all_gather | solution.py:219
  142.4 5.9 %fusion.2 = f32[512]{0:T(512)S(1)} fusion(bf16[512,4096]{1,0:T(8,128)(2,1)} %all-gather.6.cloned.1.call-done, bf16[4096,512]{1,0:T(8,128)(2,1)} %bitcast.30, f32[512]{0:T(512)S(1)} %get-tuple-element.5, f32[512]{0:T(512)S(1)} %get-tuple-element.6), kind=kOutput, calls=%fused_computation.4 | convolution fusion | flops 2148531712 | bytes 8394752 | tf_op jit(solution)/shard_map/dot_general | solution.py:220
  148.3 19.8 %all-gather.2 = f32[8,1,512]{2,1,0:T(1,128)S(1)} all-gather(f32[1,1,512]{2,1,0:T(1,128)S(1)} %bitcast.35), channel_id=3, replica_groups=mesh['section'=2,'x'=4,'z'=4,'y'=4] {'section','x'}, dimensions={0}, use_global_device_ids=true | all-gather | bytes 18432 | tf_op jit(solution)/shard_map/all_gather | solution.py:223
  168.1 0.6 dynamic_slice.11
  (3 shorter events, 0.1 us)
Async XLA Ops:
  6.5 106.5 %all-gather.8.cloned.1.call-start = ((), (), s32[]{:S(2)}) async-start(), calls=%async_computation.4 | async-start | bytes 4456448 | tf_op jit(solution)/shard_map/all_gather | solution.py:206
  18.6 123.8 %all-gather.6.cloned.1.call-start = ((), (), s32[]{:S(2)}) async-start(), calls=%async_computation.3 | async-start | bytes 4718592 | tf_op jit(solution)/shard_map/all_gather | solution.py:219
Sparse Core Ops, SparseCore 0:
  18.8 55.9 all-gather.7
  112.4 29.9 all-gather.5

commit v2 on v1

--- a/solution.py
+++ b/solution.py
@@ -194,6 +194,186 @@
     return key.reshape(t, p * n)
 
 
+MESH = pl.DeviceIdType.MESH
+C = 4
+(FAR_A, FAR_B, SUM_A, SUM_B, NEAR_A, NEAR_B, Z1, Z2, Z3, XR, XL, FWD_A, FWD_B, OWN_S, LEFT_S, RIGHT_S, FAR_SA, FAR_SB) = range(18)
+KINDS = 18
+
+
+def dense_kernel(part, w, bias, scale, out, mid_a, mid_b, from_l, from_r, pooled, feats, acc, plog, lrecv, ssem, rsem, lsend, lrec):
+    s = lax.axis_index("section")
+    x = lax.axis_index("x")
+    z = lax.axis_index("z")
+    y = lax.axis_index("y")
+    right_y, left_y, far_y = lax.rem(y + 1, 4), lax.rem(y + 3, 4), lax.rem(y + 2, 4)
+    right_x, left_x, far_x = lax.rem(x + 1, 4), lax.rem(x + 3, 4), lax.rem(x + 2, 4)
+    other = 1 - s
+
+    barrier = pltpu.get_barrier_semaphore()
+    peers = [{"y": right_y}, {"y": left_y}]
+    peers += [{"z": lax.rem(z + d, 4)} for d in (1, 2, 3)]
+    peers += [{"x": lax.rem(x + d, 4)} for d in (1, 2, 3)]
+    peers += [{"section": other}]
+    peers += [{"section": other, "x": lax.rem(x + d, 4)} for d in (1, 2, 3)]
+    for peer in peers:
+        pl.semaphore_signal(barrier, inc=1, device_id=peer, device_id_type=MESH)
+    pl.semaphore_wait(barrier, len(peers))
+
+    def remote(src, dst, kind, c, peer):
+        return pltpu.make_async_remote_copy(
+            src_ref=src, dst_ref=dst, send_sem=ssem.at[kind, c], recv_sem=rsem.at[kind, c],
+            device_id=peer, device_id_type=MESH,
+        )
+
+    A, B = pl.ds(0, 2), pl.ds(2, 2)
+    copies = []
+    for c in range(C):
+        one = {
+            FAR_A: remote(part.at[c, A, far_y], mid_a.at[c], FAR_A, c, {"y": right_y}),
+            FAR_B: remote(part.at[c, B, far_y], mid_b.at[c], FAR_B, c, {"y": left_y}),
+            SUM_A: remote(mid_a.at[c], from_l.at[c, A], SUM_A, c, {"y": right_y}),
+            SUM_B: remote(mid_b.at[c], from_r.at[c, B], SUM_B, c, {"y": left_y}),
+            NEAR_B: remote(part.at[c, B, right_y], from_l.at[c, B], NEAR_B, c, {"y": right_y}),
+            NEAR_A: remote(part.at[c, A, left_y], from_r.at[c, A], NEAR_A, c, {"y": left_y}),
+            XR: remote(feats.at[s, x, c], feats.at[s, x, c], XR, c, {"x": right_x}),
+            XL: remote(feats.at[s, x, c], feats.at[s, x, c], XL, c, {"x": left_x}),
+            FWD_A: remote(feats.at[s, left_x, c, A], feats.at[s, left_x, c, A], FWD_A, c, {"x": right_x}),
+            FWD_B: remote(feats.at[s, right_x, c, B], feats.at[s, right_x, c, B], FWD_B, c, {"x": left_x}),
+            OWN_S: remote(feats.at[s, x, c], feats.at[s, x, c], OWN_S, c, {"section": other}),
+            LEFT_S: remote(feats.at[s, left_x, c], feats.at[s, left_x, c], LEFT_S, c, {"section": other}),
+            RIGHT_S: remote(feats.at[s, right_x, c], feats.at[s, right_x, c], RIGHT_S, c, {"section": other}),
+            FAR_SA: remote(feats.at[s, far_x, c, A], feats.at[s, far_x, c, A], FAR_SA, c, {"section": other}),
+            FAR_SB: remote(feats.at[s, far_x, c, B], feats.at[s, far_x, c, B], FAR_SB, c, {"section": other}),
+        }
+        for i, kind in enumerate((Z1, Z2, Z3)):
+            to = lax.rem(z + i + 1, 4)
+            one[kind] = remote(pooled.at[c, to], feats.at[s, x, c, z], kind, c, {"z": to})
+        copies.append(one)
+
+    def start(c, *kinds):
+        for kind in kinds:
+            copies[c][kind].start()
+
+    def arrive(c, *kinds):
+        for kind in kinds:
+            copies[c][kind].wait_recv()
+
+    def stage_far(c):
+        start(c, FAR_A, FAR_B)
+
+    def stage_sum(c):
+        arrive(c, FAR_A)
+        mid_a[c] = (mid_a[c].astype(jnp.float32) + part[c, 0:2, right_y].astype(jnp.float32)).astype(jnp.bfloat16)
+        start(c, SUM_A)
+        arrive(c, FAR_B)
+        mid_b[c] = (mid_b[c].astype(jnp.float32) + part[c, 2:4, left_y].astype(jnp.float32)).astype(jnp.bfloat16)
+        start(c, SUM_B)
+        start(c, NEAR_B, NEAR_A)
+        if c + 2 < C:
+            stage_far(c + 2)
+
+    def stage_pool(c):
+        arrive(c, SUM_A, NEAR_B, SUM_B, NEAR_A)
+        total = part[c, :, y].astype(jnp.float32) + from_l[c].astype(jnp.float32) + from_r[c].astype(jnp.float32)
+        pooled[c] = total.astype(jnp.bfloat16)
+        start(c, Z1, Z3, Z2)
+        feats[s, x, c, z] = pooled[c, z]
+
+    def stage_x(c):
+        arrive(c, Z1, Z3, Z2)
+        start(c, XR, XL, OWN_S)
+
+    def stage_fwd(c):
+        arrive(c, XR)
+        start(c, FWD_A, LEFT_S)
+        arrive(c, XL)
+        start(c, FWD_B, RIGHT_S)
+
+    def stage_far_s(c):
+        arrive(c, FWD_A)
+        start(c, FAR_SA)
+        arrive(c, FWD_B)
+        start(c, FAR_SB)
+
+    def stage_dense(c):
+        arrive(c, OWN_S, LEFT_S, RIGHT_S, FAR_SA, FAR_SB)
+        acc[...] = jnp.zeros_like(acc)
+
+        @pl.loop(0, 8)
+        def _(i):
+            k0 = pl.multiple_of(i * 512, 512)
+            si, xi = i // 4, lax.rem(i, 4)
+            lhs = jnp.concatenate([feats[si, xi, c, j] for j in range(4)], axis=1)
+            acc[...] += jnp.dot(lhs, w[pl.ds(k0, 512), :], preferred_element_type=jnp.float32)
+
+        h = jnp.maximum(acc[...] + bias[...], 0.0) * scale[...]
+        h = h[:, 0:128] + h[:, 128:256] + h[:, 256:384] + h[:, 384:512]
+        plog[c] = jnp.sum(h.T, axis=0, keepdims=True)
+
+    stage_far(0)
+    stage_far(1)
+    stages = (stage_sum, stage_pool, stage_x, stage_fwd, stage_far_s, stage_dense)
+    for step in range(C + len(stages) - 1):
+        for i, stage in enumerate(stages):
+            if 0 <= step - i < C:
+                stage(step - i)
+
+    sent = []
+    for ds in range(2):
+        for dx in range(4):
+            if ds == 0 and dx == 0:
+                continue
+            to_s = s if ds == 0 else other
+            to_x = lax.rem(x + dx, 4)
+            k = ds * 4 + dx
+            copy = pltpu.make_async_remote_copy(
+                src_ref=plog.at[to_x], dst_ref=lrecv.at[s * 4 + x], send_sem=lsend.at[k], recv_sem=lrec.at[k],
+                device_id={"section": to_s, "x": to_x}, device_id_type=MESH,
+            )
+            copy.start()
+            sent.append(copy)
+    lrecv[s * 4 + x] = plog[x]
+    for copy in sent:
+        copy.wait_recv()
+    total = lrecv[0]
+    for i in range(1, 8):
+        total = total + lrecv[i]
+    out[...] = total
+    for copy in sent:
+        copy.wait_send()
+    for c in range(C):
+        for kind in range(KINDS):
+            copies[c][kind].wait_send()
+
+
+def dense(partial, w, bias, scale):
+    bf = jnp.bfloat16
+    vmem = pl.BlockSpec(memory_space=pltpu.VMEM)
+    return pl.pallas_call(
+        dense_kernel,
+        out_shape=jax.ShapeDtypeStruct((1, 128), jnp.float32),
+        in_specs=[vmem] * 4,
+        out_specs=vmem,
+        scratch_shapes=[
+            pltpu.VMEM((C, 2, 128, 128), bf),
+            pltpu.VMEM((C, 2, 128, 128), bf),
+            pltpu.VMEM((C, 4, 128, 128), bf),
+            pltpu.VMEM((C, 4, 128, 128), bf),
+            pltpu.VMEM((C, 4, 128, 128), bf),
+            pltpu.VMEM((2, 4, C, 4, 128, 128), bf),
+            pltpu.VMEM((128, 512), jnp.float32),
+            pltpu.VMEM((C, 1, 128), jnp.float32),
+            pltpu.VMEM((8, 1, 128), jnp.float32),
+            pltpu.SemaphoreType.DMA((KINDS, C)),
+            pltpu.SemaphoreType.DMA((KINDS, C)),
+            pltpu.SemaphoreType.DMA((8,)),
+            pltpu.SemaphoreType.DMA((8,)),
+        ],
+        compiler_params=pltpu.CompilerParams(collective_id=1, has_side_effects=True, vmem_limit_bytes=48 << 20),
+        cost_estimate=pl.CostEstimate(flops=3 * 10**10, bytes_accessed=10**7, transcendentals=0),
+    )(partial.reshape(4, 4, 4, 128, 128), w, bias, scale)
+
+
 ALL = ("section", "x", "z", "y")
 
 
@@ -212,17 +392,7 @@
     lists = jnp.transpose(lists, (1, 0, 2)).reshape(128, CAP)
     keys = lax.all_to_all(lists, ALL, split_axis=0, concat_axis=0, tiled=True)
     partial = lookup(keys, tables)
-    ordered = jnp.transpose(partial.reshape(64, 2, BAGS, 128), (1, 0, 2, 3)).reshape(SRC, BAGS, 128)
-    received = lax.all_to_all(ordered, ALL, split_axis=0, concat_axis=0, tiled=True)
-    pooled = jnp.sum(received.reshape(TABLES, 4, BAGS, 128).astype(jnp.float32), axis=1)
-    features = jnp.transpose(pooled.astype(jnp.bfloat16), (1, 0, 2)).reshape(BAGS, TABLES * 128)
-    samples = lax.all_gather(features, ("x", "section"), axis=0, tiled=True)
-    pre_act = jnp.dot(samples, w_all, preferred_element_type=jnp.float32)
-    hidden = jnp.maximum(pre_act + bias[None, :], 0.0)
-    logit_part = jnp.sum(hidden * scale[None, :], axis=1)
-    parts = lax.all_gather(logit_part, ("section", "x"))
-    total = jnp.sum(parts, axis=0)
-    return lax.dynamic_slice(total, (x * 128,), (128,))
+    return dense(partial, w_all, bias[None, :], scale[None, :]).reshape(128)
 
 
 def solution(mesh):

time: 176 us -> 132 us (0.75)
  blocking collectives: 86.8 us -> 10.3 us
  Pallas kernels: 32 us -> 81.8 us
  waiting for transfers between devices: 24.4 us -> 10 us
  starting transfers between devices: 0.04 us -> 10.2 us
  local copies, waits for them, and re-layouts: 10.7 us -> 4.4 us
  matrix products: 5.86 us -> 0 us
    all_to_all x2 -> x0, blocking collectives: 56.8 us -> none  [the longest x1 36 us: body(): lax.all_to_all(ordered, ALL, split_axis=0, concat_axis=0, tiled=True)]
    pallas_call x0 -> x1, Pallas kernels: none -> 47.6 us  [dense(): pl.pallas_call(dense_kernel, out_shape=jax.ShapeDtypeStruct((1, 128), jnp...]
    all_gather x1 -> x0, waiting for transfers between devices: 24.4 us -> none  [body(): samples = lax.all_gather(features, ('x', 'section'), axis=0, tiled=True)]
    all_gather x1 -> x0, blocking collectives: 19.8 us -> none  [body(): parts = lax.all_gather(logit_part, ('section', 'x'))]
    all_to_all x0 -> x1, starting transfers between devices: none -> 10.2 us  [body(): keys = lax.all_to_all(lists, ALL, split_axis=0, concat_axis=0, tiled=True)]
    all_to_all x0 -> x1, waiting for transfers between devices: none -> 10 us  [body(): keys = lax.all_to_all(lists, ALL, split_axis=0, concat_axis=0, tiled=True)]
    dot_general x1 -> x0, matrix products: 5.86 us -> none  [body(): pre_act = jnp.dot(samples, w_all, preferred_element_type=jnp.float32)]
    all_gather x1 -> x0, local copies, waits for them, and re-layouts: 5 us -> none  [body(): w_all = lax.all_gather(w_part.reshape(4, 64, quarter), ('z', 'y'), axis=1)]
  transfers between devices with their start and end apart: 2 -> 2, of which waited for: 1 -> 1; matrix products, arithmetic and copies ran while one was open for 6% -> 3% of each run, Pallas kernels for 18% -> 26%
where the time goes in v2:
time: 132 us
  Pallas kernels  81.8 us (62%)
  between operations  13.5 us (10%)
  blocking collectives  10.3 us (8%)
  starting transfers between devices  10.2 us (8%)
  waiting for transfers between devices  10 us (8%)
  local copies, waits for them, and re-layouts  4.4 us (3%)
  other arithmetic  1.79 us (1%)
    pallas_call x1, Pallas kernels, dense(): pl.pallas_call(dense_kernel, out_shape=jax.ShapeDtypeStruct((1, 128), jnp...  47.6 us
    pallas_call x1, Pallas kernels, lookup(): pl.pallas_call(lookup_kernel, out_shape=jax.ShapeDtypeStruct((SRC, BAGS,...  28.9 us
    all_to_all x1, blocking collectives, body(): lax.all_to_all(w_first, 'x', split_axis=1, concat_axis=0, tiled=True)  10.3 us
    all_to_all x1, starting transfers between devices, body(): keys = lax.all_to_all(lists, ALL, split_axis=0, concat_axis=0, tiled=True)  10.2 us
    all_to_all x1, waiting for transfers between devices, body(): keys = lax.all_to_all(lists, ALL, split_axis=0, concat_axis=0, tiled=True)  10 us
    pallas_call x1, Pallas kernels, prep(): pl.pallas_call(prep_kernel, out_shape=jax.ShapeDtypeStruct((4, TABLES, CA...  5.38 us
  transfers between devices with their start and end apart: 2, of which 1 were waited for; matrix products, arithmetic and copies ran while one was open for 3% of the time, Pallas kernels for 26%

profile of v2, /device:TPU:1, one launch (start us, length us, event | category | flops | bytes accessed | tf_op | source)
XLA Modules:
  0.0 132.0 jit_solution(15764350379453645213)
XLA Ops:
  6.5 0.0 all-gather.3.cloned.1.call-start
  6.5 1.0 copy.17
  7.5 10.3 %all_to_all.28 = bf16[64,4,512]{2,0,1:T(8,128)(2,1)} all-to-all(bf16[64,4,512]{2,0,1:T(8,128)(2,1)S(1)} %bitcast.23), channel_id=1, replica_groups=mesh['section'=2,'x'=4,'z'=4,'y'=4] {'x'}, dimensions={1} | all-to-all | bytes 524288 | tf_op jit(solution)/shard_map/all_to_all | solution.py:385
  17.8 0.0 all-gather.3.cloned.1.call-update
  17.8 1.0 bitcast_select_fusion
  18.9 0.7 reshape.21.keys
  19.6 5.4 %shard_map.64 = s32[4,32,512]{2,1,0:T(8,128)} custom-call(s32[32,512]{1,0:T(8,128)} %reshape.21.keys), custom_call_target="tpu_custom_call" | custom-call | tf_op jit(solution)/shard_map/pallas_call | solution.py:179
  24.9 1.1 copy.10
  26.1 1.1 all_to_all.25
  27.1 10.2 %all-to-all-start = ((s32[128,1,512]{2,1,0:T(1,128)}), s32[128,1,512]{2,1,0:T(1,128)S(1)}, u32[]{:S(2)}, u32[]{:S(2)}) async-start(s32[128,1,512]{2,1,0:T(1,128)} %all_to_all.25), calls=%async_computation | async-start | bytes 524288 | tf_op jit(solution)/shard_map/all_to_all | solution.py:393
  37.4 0.8 dynamic-slice_convert_fusion
  38.1 10.0 %all-to-all-done = s32[128,1,512]{2,1,0:T(1,128)S(1)} async-done(((s32[128,1,512]{2,1,0:T(1,128)}), s32[128,1,512]{2,1,0:T(1,128)S(1)}, u32[]{:S(2)}, u32[]{:S(2)}) %all-to-all-start) | async-done | bytes 262176 | tf_op jit(solution)/shard_map/all_to_all | solution.py:393
  48.2 28.9 %shard_map.65 = bf16[128,64,128]{2,1,0:T(8,128)(2,1)S(1)} custom-call(s32[128,512]{1,0:T(8,128)S(1)} %bitcast.16, bf16[32768,128]{1,0:T(8,128)(2,1)} %table.1), custom_call_target="tpu_custom_call" | custom-call | flops 10000000000 | bytes 10000000 | tf_op jit(solution)/shard_map/pallas_call | solution.py:96
  77.0 0.0 all-gather.3.cloned.1.call-done
  77.1 47.6 %shard_map.66 = f32[1,128]{1,0:T(1,128)S(1)} custom-call(bf16[4,4,4,128,128]{4,3,2,1,0:T(8,128)(2,1)S(1)} %bitcast.19, bf16[4096,512]{1,0:T(8,128)(2,1)} %bitcast.25, f32[1,512]{1,0:T(1,128)S(1)} %bitcast.18, f32[1,512]{1,0:T(1,128)S(1)} %bitcast.17), custom_call_target="tpu_custom_call" | custom-call | flops 30000001024 | bytes 10000000 | tf_op jit(solution)/shard_map/pallas_call | solution.py:352
  124.7 0.5 copy.20
  (2 shorter events, 0.0 us)
Async XLA Ops:
  6.5 70.5 %all-gather.3.cloned.1.call-start = ((), (), s32[]{:S(2)}) async-start(), calls=%async_computation.2 | async-start | bytes 4456448 | tf_op jit(solution)/shard_map/all_gather | solution.py:386
  27.1 21.0 %all-to-all-start = ((s32[128,1,512]{2,1,0:T(1,128)}), s32[128,1,512]{2,1,0:T(1,128)S(1)}, u32[]{:S(2)}, u32[]{:S(2)}) async-start(s32[128,1,512]{2,1,0:T(1,128)} %all_to_all.25), calls=%async_computation | async-start | bytes 524288 | tf_op jit(solution)/shard_map/all_to_all | solution.py:393
Sparse Core Ops, SparseCore 0:
  17.9 55.1 all-gather.2

commit v3 on v2

--- a/solution.py
+++ b/solution.py
@@ -9,107 +9,124 @@
 
 TABLES = 32
 SRC, BAGS, CAP = 128, 64, 512
-CUTS = ((64, 32, 32), (16, 16, 16, 16, 32, 32), (32,) * 4)
+TAIL = (16, 16, 16, 16, 32, 32)
 G = 8
 TB = 2048
 NBUF = 4
 
-def lookup_kernel(keys, table, out, rows_v, rows_s, tab, stage, buf, sem_s, sem_t):
-    nb = table.shape[0] // TB
-    def fetch(i, slot):
-        return pltpu.make_async_copy(table.at[pl.ds(i * TB, TB), :], stage.at[slot], sem_t.at[slot])
-    for i in range(NBUF):
-        fetch(i, i).start()
-    k = keys[...]
-    n = jnp.sum((k < (BAGS << 15)).astype(jnp.int32), axis=1, keepdims=True)
-    for r in range(4):
-        rows_v[r * SRC:(r + 1) * SRC, :] = k[:, r * 128:(r + 1) * 128] & 32767
-    rows_v[4 * SRC:, :] = jnp.broadcast_to(n, (SRC, 128))
-    cps = [pltpu.make_async_copy(rows_v.at[pl.ds(i * SRC, SRC), :], rows_s.at[pl.ds(i * SRC, SRC), :], sem_s.at[i]) for i in range(5)]
-    cps[4].start()
-    cps[0].start()
-    cps[1].start()
+
+def lookup_kernel(lists, tab, out, keys, rows_v, n_v, rows_s, n_s, buf, sem_n, sem_r, sem_f):
+    y = lax.axis_index("y")
+    lane = lax.broadcasted_iota(jnp.int32, (SRC, LANES), 1)
+    blocks = [lists[:, b * LANES:(b + 1) * LANES] for b in range(BLKS)]
+    first = sum(jnp.sum((v < (y << 21)).astype(jnp.int32), axis=1, keepdims=True) for v in blocks)
+    blocks = rotate_left(blocks, lane, jnp.broadcast_to(first, (SRC, LANES)))
+    n = jnp.zeros((SRC, 1), jnp.int32)
+    for b in range(BLKS):
+        mine = (blocks[b] >> 21) == y
+        n += jnp.sum(mine.astype(jnp.int32), axis=1, keepdims=True)
+        keys[:, b * LANES:(b + 1) * LANES] = jnp.where(mine, (blocks[b] >> 15) & 63, BAGS)
+        rows_v[b] = jnp.where(mine, blocks[b] & 32767, 0)
+    n_v[...] = jnp.broadcast_to(n, (SRC, LANES)).T[0:8]
+    n_copy = pltpu.make_async_copy(n_v, n_s, sem_n)
+    n_copy.start()
+
+    def tile(r, grp, slot, sem):
+        rows = pl.ds(pl.multiple_of(grp * G, G), G)
+        return pltpu.make_async_copy(rows_v.at[r, rows, :], rows_s.at[slot, r], sem)
+
+    for r in range(2):
+        tile(r, 0, 0, sem_r.at[0, r]).start()
     buf[...] = jnp.zeros_like(buf)
-
-    @pl.loop(0, nb // NBUF)
-    def _(h):
-        for slot in range(NBUF):
-            i = h * NBUF + slot
-            fetch(i, slot).wait()
-            base = pl.multiple_of(i * TB, TB)
-            tab[pl.ds(base, TB), :] = stage[slot].astype(jnp.float32)
-            @pl.when(i + NBUF < nb)
-            def _():
-                fetch(i + NBUF, slot).start()
-
-    cps[4].wait()
-    cps[0].wait()
-    cps[1].wait()
-    most = lax.fori_loop(0, SRC, lambda c, m: jnp.maximum(m, rows_s[4 * SRC + c, 0]), 0, unroll=False)
-    @pl.when(most > 256)
-    def _():
-        cps[2].start()
-        cps[3].start()
-        cps[2].wait()
-        cps[3].wait()
+    n_copy.wait()
+
     bag_row = lax.broadcasted_iota(jnp.int32, (BAGS, 256), 0)
 
-    @pl.loop(0, SRC // G)
-    def _(grp):
-        @pl.loop(0, G)
-        def _(g):
-            c = grp * G + g
-            n = rows_s[4 * SRC + c, 0]
-            for r in range(4):
-                def some(r=r):
-                    view = rows_s.at[r * SRC + c]
-                    at = 0
-                    for size in CUTS[min(r, 2)]:
-                        def block(at=at, size=size):
-                            for u in range(at, at + size):
-                                buf[g, r * 128 + u: r * 128 + u + 1, :] = tab[pl.ds(view[u], 1), :]
-                        if at == 0:
-                            block()
-                        else:
-                            pl.when(n > r * 128 + at)(block)
-                        at += size
-                if r == 0:
-                    some()
-                else:
-                    pl.when(n > r * 128)(some)
-        def part(g, lo):
-            kk = keys[pl.ds(grp * G + g, 1), lo:lo + 256] >> 15
-            oh = jnp.where(kk == bag_row, 1.0, 0.0).astype(jnp.bfloat16)
-            return jnp.dot(oh, buf[g, lo:lo + 256, :].astype(jnp.bfloat16), preferred_element_type=jnp.float32)
-        most = rows_s[4 * SRC + grp * G, 0]
+    def part(grp, slot, g, lo):
+        kk = keys[pl.ds(grp * G + g, 1), lo:lo + 256]
+        oh = jnp.where(kk == bag_row, 1.0, 0.0).astype(jnp.bfloat16)
+        return jnp.dot(oh, buf[slot, g, lo:lo + 256, :].astype(jnp.bfloat16), preferred_element_type=jnp.float32)
+
+    def place(grp, g):
+        return ((grp >> 1) & 1) * 64 + (grp & 1) * 8 + (grp >> 2) + (g % 4) * 16 + (g // 4) * 4
+
+    def pool(grp, slot):
+        for g in range(G):
+            out[place(grp, g)] = part(grp, slot, g, 0).astype(jnp.bfloat16)
+
+    def long_lists(grp, slot):
+        most = n_s[0, grp * G]
         for g in range(1, G):
-            most = jnp.maximum(most, rows_s[4 * SRC + grp * G + g, 0])
-        for g in range(G):
-            out[grp * G + g] = part(g, 0).astype(jnp.bfloat16)
+            most = jnp.maximum(most, n_s[0, grp * G + g])
+
         @pl.when(most > 256)
         def _():
+            for r in (2, 3):
+                copy = tile(r, grp, slot, sem_f)
+                copy.start()
+                copy.wait()
+
             for g in range(G):
-                out[grp * G + g] = (part(g, 0) + part(g, 256)).astype(jnp.bfloat16)
-
-
-def lookup(keys, table):
+                for r in (2, 3):
+                    @pl.loop(0, 128)
+                    def _(u):
+                        buf[slot, g, pl.ds(r * 128 + u, 1), :] = tab[pl.ds(rows_s[slot, r, g, u], 1), :]
+                total = part(grp, slot, g, 0) + part(grp, slot, g, 256)
+                out[place(grp, g)] = total.astype(jnp.bfloat16)
+
+    @pl.loop(0, SRC // G // 2)
+    def _(h):
+        for slot in range(2):
+            grp = h * 2 + slot
+            for r in range(2):
+                tile(r, grp, slot, sem_r.at[slot, r]).wait()
+
+            @pl.when(grp + 1 < SRC // G)
+            def _():
+                for r in range(2):
+                    tile(r, grp + 1, 1 - slot, sem_r.at[1 - slot, r]).start()
+
+            before = jnp.maximum(grp - 1, 0)
+            for g in range(G):
+                for u in range(128):
+                    buf[slot, g, u:u + 1, :] = tab[pl.ds(rows_s[slot, 0, g, u], 1), :]
+            pool(before, 1 - slot)
+            for g in range(G):
+                count = n_s[0, grp * G + g]
+                at = 0
+                for size in TAIL:
+                    @pl.when(count > 128 + at)
+                    def _(at=at, size=size):
+                        for u in range(at, at + size):
+                            buf[slot, g, 128 + u:129 + u, :] = tab[pl.ds(rows_s[slot, 1, g, u], 1), :]
+                    at += size
+            long_lists(before, 1 - slot)
+
+    pool(SRC // G - 1, 1)
+    long_lists(SRC // G - 1, 1)
+
+
+def lookup(lists, tab):
+    vmem = pl.BlockSpec(memory_space=pltpu.VMEM)
     return pl.pallas_call(
         lookup_kernel,
-        out_shape=jax.ShapeDtypeStruct((SRC, BAGS, 128), jnp.bfloat16),
-        in_specs=[pl.BlockSpec(memory_space=pltpu.VMEM), pl.BlockSpec(memory_space=pl.ANY)],
-        out_specs=pl.BlockSpec(memory_space=pltpu.VMEM),
+        out_shape=pltpu.VMEM((SRC, BAGS, 128), jnp.bfloat16),
+        in_specs=[vmem, vmem],
+        out_specs=vmem,
         scratch_shapes=[
-            pltpu.VMEM((SRC * 5, 128), jnp.int32),
-            pltpu.SMEM((SRC * 5, 128), jnp.int32),
-            pltpu.VMEM((table.shape[0], 128), jnp.float32),
-            pltpu.VMEM((NBUF, TB, 128), jnp.bfloat16),
-            pltpu.VMEM((G, CAP, 128), jnp.float32),
-            pltpu.SemaphoreType.DMA((5,)),
-            pltpu.SemaphoreType.DMA((NBUF,)),
+            pltpu.VMEM((SRC, CAP), jnp.int32),
+            pltpu.VMEM((4, SRC, 128), jnp.int32),
+            pltpu.VMEM((8, 128), jnp.int32),
+            pltpu.SMEM((2, 4, G, 128), jnp.int32),
+            pltpu.SMEM((8, 128), jnp.int32),
+            pltpu.VMEM((2, G, CAP, 128), jnp.float32),
+            pltpu.SemaphoreType.DMA,
+            pltpu.SemaphoreType.DMA((2, 2)),
+            pltpu.SemaphoreType.DMA,
         ],
-        compiler_params=pltpu.CompilerParams(vmem_limit_bytes=48 << 20),
+        compiler_params=pltpu.CompilerParams(vmem_limit_bytes=32 << 20),
         cost_estimate=pl.CostEstimate(flops=10**10, bytes_accessed=10**7, transcendentals=0),
-    )(keys, table)
+    )(lists, tab)
 
 
 LANES = 128
@@ -162,26 +179,164 @@
         s *= 2
     return xs
 
-def prep_kernel(keys, out):
+WZR, WZL, WYR, WYL, WFZR, WFZL, WFYR, WFYL = range(8)
+
+
+def front_kernel(keys, w, table, lists, w_a, w_b, tab, own, from_x, to_z, from_z, both, stage, xs, xr, ls, lr, gs, gr, sem_t):
+    s = lax.axis_index("section")
+    x = lax.axis_index("x")
+    z = lax.axis_index("z")
+    y = lax.axis_index("y")
+    other = 1 - s
+    nb = table.shape[0] // TB
+
+    def fetch(i, slot):
+        return pltpu.make_async_copy(table.at[pl.ds(i * TB, TB), :], stage.at[slot], sem_t.at[slot])
+
+    for i in range(NBUF):
+        fetch(i, i).start()
+
+    def widen(h):
+        @pl.loop(h * (nb // NBUF) // 4, (h + 1) * (nb // NBUF) // 4)
+        def _(k):
+            for slot in range(NBUF):
+                i = k * NBUF + slot
+                fetch(i, slot).wait()
+                tab[pl.ds(pl.multiple_of(i * TB, TB), TB), :] = stage[slot].astype(jnp.float32)
+
+                @pl.when(i + NBUF < nb)
+                def _():
+                    fetch(i + NBUF, slot).start()
+
+    barrier = pltpu.get_barrier_semaphore()
+    peers = [{"section": other}]
+    for axis, at in (("x", x), ("z", z), ("y", y)):
+        peers += [{axis: lax.rem(at + d, 4)} for d in (1, 2, 3)]
+    for peer in peers:
+        pl.semaphore_signal(barrier, inc=1, device_id=peer, device_id_type=MESH)
+
     lane = lax.broadcasted_iota(jnp.int32, (TABLES, LANES), 1)
-    xs = bitonic([keys[:, b * LANES:(b + 1) * LANES] for b in range(BLKS)], lane)
-    for j in range(4):
-        ys = xs
-        if j:
-            start = sum(jnp.sum((x < (j << 21)).astype(jnp.int32), axis=1, keepdims=True) for x in xs)
-            ys = rotate_left(xs, lane, jnp.broadcast_to(start, (TABLES, LANES)))
-        for b in range(BLKS):
-            mine = (ys[b] >> 21) == j
-            out[j, :, b * LANES:(b + 1) * LANES] = jnp.where(mine, ys[b] & ((1 << 21) - 1), 64 << 15)
-
-
-def prep(keys):
+    blocks = bitonic([keys[:, b * LANES:(b + 1) * LANES] for b in range(BLKS)], lane)
+    for b in range(BLKS):
+        own[:, :, b * LANES:(b + 1) * LANES] = blocks[b].reshape(4, 8, LANES)
+    pl.semaphore_wait(barrier, len(peers))
+
+    def list_copy(k, src, dst, peer):
+        return pltpu.make_async_remote_copy(
+            src_ref=src, dst_ref=dst, send_sem=ls.at[k], recv_sem=lr.at[k], device_id=peer, device_id_type=MESH,
+        )
+
+    sent = []
+    along_x = []
+    for i in range(3):
+        to = lax.rem(x + i + 1, 4)
+        along_x.append(list_copy(i, own.at[to], from_x.at[x], {"x": to}))
+    for copy in along_x:
+        copy.start()
+
+    x_copies = []
+    for i in range(3):
+        to = lax.rem(x + i + 1, 4)
+        for half, full, mine in ((0, w_a, z), (1, w_b, y)):
+            cols = pl.ds(pl.multiple_of(to * 512 + half * 256, 256), 256)
+            copy = pltpu.make_async_remote_copy(
+                src_ref=w.at[:, cols], dst_ref=full.at[mine, x], send_sem=xs.at[i, half], recv_sem=xr.at[i, half],
+                device_id={"x": to}, device_id_type=MESH,
+            )
+            copy.start()
+            x_copies.append(copy)
+    for half, full, mine in ((0, w_a, z), (1, w_b, y)):
+        cols = pl.ds(pl.multiple_of(x * 512 + half * 256, 256), 256)
+        full[mine, x] = w[:, cols]
+    from_x[x] = own[x]
+    widen(0)
+
+    def ring(kind, ref, axis, to):
+        return pltpu.make_async_remote_copy(
+            src_ref=ref, dst_ref=ref, send_sem=gs.at[kind], recv_sem=gr.at[kind], device_id={axis: to}, device_id_type=MESH,
+        )
+
+    z_right, z_left = lax.rem(z + 1, 4), lax.rem(z + 3, 4)
+    y_right, y_left = lax.rem(y + 1, 4), lax.rem(y + 3, 4)
+    low, high = pl.ds(0, 2), pl.ds(2, 2)
+    near = [
+        ring(WZR, w_a.at[z], "z", z_right), ring(WZL, w_a.at[z], "z", z_left),
+        ring(WYR, w_b.at[y], "y", y_right), ring(WYL, w_b.at[y], "y", y_left),
+    ]
+    far = [
+        ring(WFZR, w_a.at[z_left, low], "z", z_right), ring(WFZL, w_a.at[z_right, high], "z", z_left),
+        ring(WFYR, w_b.at[y_left, low], "y", y_right), ring(WFYL, w_b.at[y_right, high], "y", y_left),
+    ]
+    for copy in along_x:
+        copy.wait_recv()
+    for xi in range(4):
+        for si in range(2):
+            for zi in range(4):
+                to_z[zi, si * 4 + xi:si * 4 + xi + 1, :] = from_x[xi, si * 4 + zi:si * 4 + zi + 1, :]
+    along_z = []
+    for i in range(3):
+        to = lax.rem(z + i + 1, 4)
+        along_z.append(list_copy(3 + i, to_z.at[to], from_z.at[z], {"z": to}))
+    for copy in along_z:
+        copy.start()
+    from_z[z] = to_z[z]
+    for copy in x_copies:
+        copy.wait_recv()
+    for copy in near:
+        copy.start()
+    widen(1)
+
+    for copy in along_z:
+        copy.wait_recv()
+    for zi in range(4):
+        for si in range(2):
+            both[si, zi * 4:zi * 4 + 4, :] = from_z[zi, si * 4:si * 4 + 4, :]
+    across = list_copy(6, both.at[other], lists.at[y, s], {"section": other})
+    across.start()
+    along_y = []
+    for i in range(3):
+        along_y.append(list_copy(7 + i, both.at[s], lists.at[y, s], {"y": lax.rem(y + i + 1, 4)}))
+    for copy in along_y:
+        copy.start()
+    lists[y, s] = both[s]
+    across.wait_recv()
+    for i in range(3):
+        copy = list_copy(10 + i, lists.at[y, other], lists.at[y, other], {"y": lax.rem(y + i + 1, 4)})
+        copy.start()
+        along_y.append(copy)
+
+    widen(2)
+    for copy, onward in zip(near, far):
+        copy.wait_recv()
+        onward.start()
+    widen(3)
+    for copy in along_y + far:
+        copy.wait_recv()
+    for copy in along_x + along_z + [across] + along_y + x_copies + near + far:
+        copy.wait_send()
+
+
+def front(keys, w, table):
+    vmem = pl.BlockSpec(memory_space=pltpu.VMEM)
+    piece = pltpu.VMEM((4, 4, 64, 256), jnp.bfloat16)
+    rows = pltpu.VMEM((4, 8, CAP), jnp.int32)
+    dma = pltpu.SemaphoreType.DMA
     return pl.pallas_call(
-        prep_kernel,
-        out_shape=jax.ShapeDtypeStruct((4, TABLES, CAP), jnp.int32),
-        in_specs=[pl.BlockSpec(memory_space=pltpu.VMEM)],
-        out_specs=pl.BlockSpec(memory_space=pltpu.VMEM),
-    )(keys)
+        front_kernel,
+        out_shape=(
+            pltpu.VMEM((4, 2, 16, CAP), jnp.int32), piece, piece, pltpu.VMEM(table.shape, jnp.float32),
+        ),
+        in_specs=[vmem, vmem, pl.BlockSpec(memory_space=pl.ANY)],
+        out_specs=(vmem,) * 4,
+        scratch_shapes=[
+            rows, rows, rows, rows,
+            pltpu.VMEM((2, 16, CAP), jnp.int32),
+            pltpu.VMEM((NBUF, TB, 128), jnp.bfloat16),
+            dma((3, 2)), dma((3, 2)), dma((13,)), dma((13,)), dma((8,)), dma((8,)), dma((NBUF,)),
+        ],
+        compiler_params=pltpu.CompilerParams(collective_id=0, has_side_effects=True, vmem_limit_bytes=40 << 20),
+        cost_estimate=pl.CostEstimate(flops=10**10, bytes_accessed=10**7, transcendentals=0),
+    )(keys, w, table)
 
 
 def make_keys(indices, pool_len):
@@ -191,7 +346,7 @@
     idx = jnp.transpose(indices, (1, 2, 0))
     key = ((idx >> 15) << 21) | (bag << 15) | (idx & 32767)
     key = jnp.where(slot < pool_len[:, None, None], key, 4 << 21)
-    return key.reshape(t, p * n)
+    return jnp.transpose(key.reshape(2, 4, 4, p * n), (1, 0, 2, 3)).reshape(t, p * n)
 
 
 MESH = pl.DeviceIdType.MESH
@@ -200,7 +355,7 @@
 KINDS = 18
 
 
-def dense_kernel(part, w, bias, scale, out, mid_a, mid_b, from_l, from_r, pooled, feats, acc, plog, lrecv, ssem, rsem, lsend, lrec):
+def dense_kernel(part, w_a, w_b, bias, scale, out, mid_a, mid_b, from_l, from_r, pooled, feats, acc, plog, lrecv, full_a, full_b, ssem, rsem, lsend, lrec, wsend, wrecv):
     s = lax.axis_index("section")
     x = lax.axis_index("x")
     z = lax.axis_index("z")
@@ -258,6 +413,44 @@
         for kind in kinds:
             copies[c][kind].wait_recv()
 
+    right_z, left_z, far_z = lax.rem(z + 1, 4), lax.rem(z + 3, 4), lax.rem(z + 2, 4)
+
+    def w_copy(k, i, src, full, row, axis, to):
+        return pltpu.make_async_remote_copy(
+            src_ref=src.at[i] if src is not full else full.at[row, i], dst_ref=full.at[row, i],
+            send_sem=wsend.at[k, i], recv_sem=wrecv.at[k, i], device_id={axis: to}, device_id_type=MESH,
+        )
+
+    w_near, w_far = {}, {}
+    for half, (src, full, axis, mine, right, left) in enumerate(
+        ((w_a, full_a, "y", y, right_y, left_y), (w_b, full_b, "z", z, right_z, left_z))
+    ):
+        for i in range(4):
+            w_near[half, 0, i] = w_copy(half * 4, i, src, full, mine, axis, right)
+            w_near[half, 1, i] = w_copy(half * 4 + 1, i, src, full, mine, axis, left)
+        for i in range(2):
+            w_far[half, 0, i] = w_copy(half * 4 + 2, i, full, full, left, axis, right)
+            w_far[half, 1, i] = w_copy(half * 4 + 3, i + 2, full, full, right, axis, left)
+
+    def w_start(half, *pieces):
+        for i in pieces:
+            w_near[half, 0, i].start()
+            w_near[half, 1, i].start()
+
+    def w_onward(half, i):
+        w_near[half, 0, i].wait_recv()
+        w_far[half, 0, i].start()
+        w_near[half, 1, i + 2].wait_recv()
+        w_far[half, 1, i].start()
+
+    def w_arrive():
+        for half in range(2):
+            for i in range(2):
+                w_near[half, 0, i + 2].wait_recv()
+                w_near[half, 1, i].wait_recv()
+                w_far[half, 0, i].wait_recv()
+                w_far[half, 1, i].wait_recv()
+
     def stage_far(c):
         start(c, FAR_A, FAR_B)
 
@@ -295,28 +488,54 @@
         arrive(c, FWD_B)
         start(c, FAR_SB)
 
-    def stage_dense(c):
-        arrive(c, OWN_S, LEFT_S, RIGHT_S, FAR_SA, FAR_SB)
-        acc[...] = jnp.zeros_like(acc)
+    def dense_rows(first, last):
+        rows = (last - first) * 128
+        for c in range(first, last):
+            arrive(c, OWN_S, LEFT_S, RIGHT_S, FAR_SA, FAR_SB)
+        acc[0:rows] = jnp.zeros((rows, 512), jnp.float32)
 
         @pl.loop(0, 8)
         def _(i):
-            k0 = pl.multiple_of(i * 512, 512)
             si, xi = i // 4, lax.rem(i, 4)
-            lhs = jnp.concatenate([feats[si, xi, c, j] for j in range(4)], axis=1)
-            acc[...] += jnp.dot(lhs, w[pl.ds(k0, 512), :], preferred_element_type=jnp.float32)
-
-        h = jnp.maximum(acc[...] + bias[...], 0.0) * scale[...]
-        h = h[:, 0:128] + h[:, 128:256] + h[:, 256:384] + h[:, 384:512]
-        plog[c] = jnp.sum(h.T, axis=0, keepdims=True)
+            zi, wx = 2 * lax.rem(i, 2), i // 2
+            lhs = jnp.concatenate(
+                [jnp.concatenate([feats[si, xi, c, j] for j in range(4)], axis=1) for c in range(first, last)], axis=0
+            )
+            rhs_a = jnp.concatenate([full_a[yy, zi + zz, wx] for zz in range(2) for yy in range(4)], axis=0)
+            acc[0:rows, 0:256] += jnp.dot(lhs, rhs_a, preferred_element_type=jnp.float32)
+            rhs_b = jnp.concatenate([full_b[zi + zz, yy, wx] for zz in range(2) for yy in range(4)], axis=0)
+            acc[0:rows, 256:512] += jnp.dot(lhs, rhs_b, preferred_element_type=jnp.float32)
+
+        for k in range(rows // 128):
+            h = jnp.maximum(acc[k * 128:(k + 1) * 128] + bias[...], 0.0) * scale[...]
+            h = h[:, 0:128] + h[:, 128:256] + h[:, 256:384] + h[:, 384:512]
+            plog[first + k] = jnp.sum(h.T, axis=0, keepdims=True)
 
     stage_far(0)
     stage_far(1)
-    stages = (stage_sum, stage_pool, stage_x, stage_fwd, stage_far_s, stage_dense)
+    w_start(1, 0, 2)
+    full_a[y] = w_a[...]
+    full_b[z] = w_b[...]
+    stages = (stage_sum, stage_pool, stage_x, stage_fwd, stage_far_s)
     for step in range(C + len(stages) - 1):
+        if step == C + 3:
+            w_arrive()
+            dense_rows(0, 3)
         for i, stage in enumerate(stages):
             if 0 <= step - i < C:
                 stage(step - i)
+        if step == 1:
+            w_start(1, 1, 3)
+        elif step == 2:
+            w_onward(1, 0)
+        elif step == 3:
+            w_onward(1, 1)
+            w_start(0, 0, 2, 1, 3)
+        elif step == 5:
+            w_onward(0, 0)
+        elif step == 6:
+            w_onward(0, 1)
+    dense_rows(3, 4)
 
     sent = []
     for ds in range(2):
@@ -339,20 +558,20 @@
     for i in range(1, 8):
         total = total + lrecv[i]
     out[...] = total
-    for copy in sent:
+    for copy in sent + list(w_near.values()) + list(w_far.values()):
         copy.wait_send()
     for c in range(C):
         for kind in range(KINDS):
             copies[c][kind].wait_send()
 
 
-def dense(partial, w, bias, scale):
+def dense(partial, w_a, w_b, bias, scale):
     bf = jnp.bfloat16
     vmem = pl.BlockSpec(memory_space=pltpu.VMEM)
     return pl.pallas_call(
         dense_kernel,
         out_shape=jax.ShapeDtypeStruct((1, 128), jnp.float32),
-        in_specs=[vmem] * 4,
+        in_specs=[vmem] * 5,
         out_specs=vmem,
         scratch_shapes=[
             pltpu.VMEM((C, 2, 128, 128), bf),
@@ -361,17 +580,21 @@
             pltpu.VMEM((C, 4, 128, 128), bf),
             pltpu.VMEM((C, 4, 128, 128), bf),
             pltpu.VMEM((2, 4, C, 4, 128, 128), bf),
-            pltpu.VMEM((128, 512), jnp.float32),
+            pltpu.VMEM((384, 512), jnp.float32),
             pltpu.VMEM((C, 1, 128), jnp.float32),
             pltpu.VMEM((8, 1, 128), jnp.float32),
+            pltpu.VMEM((4, 4, 4, 64, 256), bf),
+            pltpu.VMEM((4, 4, 4, 64, 256), bf),
             pltpu.SemaphoreType.DMA((KINDS, C)),
             pltpu.SemaphoreType.DMA((KINDS, C)),
             pltpu.SemaphoreType.DMA((8,)),
             pltpu.SemaphoreType.DMA((8,)),
+            pltpu.SemaphoreType.DMA((8, 4)),
+            pltpu.SemaphoreType.DMA((8, 4)),
         ],
         compiler_params=pltpu.CompilerParams(collective_id=1, has_side_effects=True, vmem_limit_bytes=48 << 20),
         cost_estimate=pl.CostEstimate(flops=3 * 10**10, bytes_accessed=10**7, transcendentals=0),
-    )(partial.reshape(4, 4, 4, 128, 128), w, bias, scale)
+    )(partial.reshape(4, 4, 4, 128, 128), w_a, w_b, bias, scale)
 
 
 ALL = ("section", "x", "z", "y")
@@ -379,20 +602,12 @@
 
 def body(indices, pool_len, tables, w_first, b_first, w_out):
     x = lax.axis_index("x")
-    z = lax.axis_index("z")
-    y = lax.axis_index("y")
     quarter = w_first.shape[1] // 4
-    w_part = lax.all_to_all(w_first, "x", split_axis=1, concat_axis=0, tiled=True)
-    w_all = lax.all_gather(w_part.reshape(4, 64, quarter), ("z", "y"), axis=1)
-    w_all = w_all.reshape(-1, quarter)
     bias = lax.dynamic_slice(b_first, (x * quarter,), (quarter,)).astype(jnp.float32)
     scale = lax.dynamic_slice(w_out, (x * quarter,), (quarter,)).astype(jnp.float32)
-
-    lists = prep(make_keys(indices, pool_len))
-    lists = jnp.transpose(lists, (1, 0, 2)).reshape(128, CAP)
-    keys = lax.all_to_all(lists, ALL, split_axis=0, concat_axis=0, tiled=True)
-    partial = lookup(keys, tables)
-    return dense(partial, w_all, bias[None, :], scale[None, :]).reshape(128)
+    lists, w_a, w_b, tab = front(make_keys(indices, pool_len), w_first, tables)
+    partial = lookup(lists.reshape(SRC, CAP), tab)
+    return dense(partial, w_a, w_b, bias[None, :], scale[None, :]).reshape(128)
 
 
 def solution(mesh):

time: 132 us -> 100 us (0.76)
  Pallas kernels: 81.8 us -> 97.5 us
  between operations: 13.5 us -> 0.05 us
  blocking collectives: 10.3 us -> 0 us
  starting transfers between devices: 10.2 us -> 0 us
  waiting for transfers between devices: 10 us -> 0 us
  local copies, waits for them, and re-layouts: 4.4 us -> 1.26 us
    all_to_all x1 -> x0, blocking collectives: 10.3 us -> none  [body(): lax.all_to_all(w_first, 'x', split_axis=1, concat_axis=0, tiled=True)]
    all_to_all x1 -> x0, starting transfers between devices: 10.2 us -> none  [body(): keys = lax.all_to_all(lists, ALL, split_axis=0, concat_axis=0, tiled=True)]
    all_to_all x1 -> x0, waiting for transfers between devices: 10 us -> none  [body(): keys = lax.all_to_all(lists, ALL, split_axis=0, concat_axis=0, tiled=True)]
    pallas_call x2, Pallas kernels: 34.2 us -> 42.5 us  [the longest x1 24.2 us: front(): pl.pallas_call(front_kernel, out_shape=(pltpu.VMEM((4, 2, 16, CAP), jnp.i...]
    pallas_call x1, Pallas kernels: 47.6 us -> 55.1 us  [dense(): pl.pallas_call(dense_kernel, out_shape=jax.ShapeDtypeStruct((1, 128), jnp...]
    all_to_all x2 -> x0, local copies, waits for them, and re-layouts: 2.04 us -> none  [the longest x1 1.08 us: body(): keys = lax.all_to_all(lists, ALL, split_axis=0, concat_axis=0, tiled=True)]
  transfers between devices with their start and end apart: 2 -> 0, of which waited for: 1 -> 0; matrix products, arithmetic and copies ran while one was open for 3% -> 0% of each run, Pallas kernels for 26% -> 0%
where the time goes in v3:
time: 100 us; the launch traced here: 101 us
  Pallas kernels  97.5 us (98%)
  other arithmetic  1.78 us (2%)
  local copies, waits for them, and re-layouts  1.26 us (1%)
    pallas_call x1, Pallas kernels, dense(): pl.pallas_call(dense_kernel, out_shape=jax.ShapeDtypeStruct((1, 128), jnp...  55.1 us
    pallas_call x1, Pallas kernels, front(): pl.pallas_call(front_kernel, out_shape=(pltpu.VMEM((4, 2, 16, CAP), jnp.i...  24.2 us
    pallas_call x1, Pallas kernels, lookup(): pl.pallas_call(lookup_kernel, out_shape=pltpu.VMEM((SRC, BAGS, 128), jnp....  18.3 us

profile of v3, /device:TPU:1, one launch (start us, length us, event | category | flops | bytes accessed | tf_op | source)
XLA Modules:
  0.0 100.6 jit_solution(9690522495304810002)
XLA Ops:
  0.0 1.0 bitcast_select_fusion
  1.0 0.1 reshape.16
  1.1 0.6 reshape.17.keys
  1.8 24.2 %shard_map.64 = (s32[4,2,16,512]{3,2,1,0:T(8,128)S(1)}, bf16[4,4,64,256]{3,2,1,0:T(8,128)(2,1)S(1)}, bf16[4,4,64,256]{3,2,1,0:T(8,128)(2,1)S(1)}, f32[32768,128]{1,0:T(8,128)S(1)}) custom-call(s32[32,512]{1,0:T(8,128)} %reshape.17.keys, bf16[64,2048]{1,0:T(8,128)(2,1)} %w.1, bf16[32768,128]{1,0:T(8,128)(2,1)} %table.1), custom_call_target="tpu_custom_call" | custom-call | flops 10000000000 | bytes 10000000 | tf_op jit(solution)/shard_map/pallas_call | solution.py:324
  25.9 18.3 %shard_map.65 = bf16[128,64,128]{2,1,0:T(8,128)(2,1)S(1)} custom-call(s32[128,512]{1,0:T(8,128)S(1)} %bitcast.13, f32[32768,128]{1,0:T(8,128)S(1)} %get-tuple-element.10.tab), custom_call_target="tpu_custom_call" | custom-call | flops 10000000000 | bytes 10000000 | tf_op jit(solution)/shard_map/pallas_call | solution.py:111
  44.2 0.8 dynamic-slice_convert_fusion
  45.0 55.1 %shard_map.66 = f32[1,128]{1,0:T(1,128)S(1)} custom-call(bf16[4,4,4,128,128]{4,3,2,1,0:T(8,128)(2,1)S(1)} %bitcast.12, bf16[4,4,64,256]{3,2,1,0:T(8,128)(2,1)S(1)} %get-tuple-element.11.w_a, bf16[4,4,64,256]{3,2,1,0:T(8,128)(2,1)S(1)} %get-tuple-element.12.w_b, f32[1,512]{1,0:T(1,128)S(1)} %bitcast.11, f32[1,512]{1,0:T(1,128)S(1)} %bitcast.10), custom_call_target="tpu_custom_call" | custom-call | flops 30000001024 | bytes 10000000 | tf_op jit(solution)/shard_map/pallas_call | solution.py:571
  100.1 0.5 copy.11
  (2 shorter events, 0.0 us)

commit v4 on v3

--- a/solution.py
+++ b/solution.py
@@ -124,7 +124,7 @@
             pltpu.SemaphoreType.DMA((2, 2)),
             pltpu.SemaphoreType.DMA,
         ],
-        compiler_params=pltpu.CompilerParams(vmem_limit_bytes=32 << 20),
+        compiler_params=pltpu.CompilerParams(vmem_limit_bytes=10 << 20),
         cost_estimate=pl.CostEstimate(flops=10**10, bytes_accessed=10**7, transcendentals=0),
     )(lists, tab)
 
@@ -182,7 +182,7 @@
 WZR, WZL, WYR, WYL, WFZR, WFZL, WFYR, WFYL = range(8)
 
 
-def front_kernel(keys, w, table, lists, w_a, w_b, tab, own, from_x, to_z, from_z, both, stage, xs, xr, ls, lr, gs, gr, sem_t):
+def front_kernel(indices, pool_len, w, table, lists, w_a, w_b, tab, own, from_x, to_z, from_z, both, stage, xs, xr, ls, lr, gs, gr, sem_t):
     s = lax.axis_index("section")
     x = lax.axis_index("x")
     z = lax.axis_index("z")
@@ -216,9 +216,21 @@
         pl.semaphore_signal(barrier, inc=1, device_id=peer, device_id_type=MESH)
 
     lane = lax.broadcasted_iota(jnp.int32, (TABLES, LANES), 1)
-    blocks = bitonic([keys[:, b * LANES:(b + 1) * LANES] for b in range(BLKS)], lane)
+    row = lax.broadcasted_iota(jnp.int32, (TABLES, TABLES), 0)
+    column = lax.broadcasted_iota(jnp.int32, (TABLES, TABLES), 1)
+    used = jnp.sum(jnp.where(row == column, jnp.broadcast_to(pool_len[...], (TABLES, TABLES)), 0), axis=1, keepdims=True)
+    blocks = []
     for b in range(BLKS):
-        own[:, :, b * LANES:(b + 1) * LANES] = blocks[b].reshape(4, 8, LANES)
+        idx = jnp.concatenate([indices[:, 2 * b, :], indices[:, 2 * b + 1, :]], axis=1)
+        slot = 2 * b + (lane >> 6)
+        key = ((idx >> 15) << 21) | ((lane & 63) << 15) | (idx & 32767)
+        blocks.append(jnp.where(slot < used, key, 4 << 21))
+    blocks = bitonic(blocks, lane)
+    for b in range(BLKS):
+        for xi in range(4):
+            for si in range(2):
+                t = si * 16 + xi * 4
+                own[xi, si * 4:si * 4 + 4, b * LANES:(b + 1) * LANES] = blocks[b][t:t + 4]
     pl.semaphore_wait(barrier, len(peers))
 
     def list_copy(k, src, dst, peer):
@@ -316,7 +328,7 @@
         copy.wait_send()
 
 
-def front(keys, w, table):
+def front(indices, pool_len, w, table):
     vmem = pl.BlockSpec(memory_space=pltpu.VMEM)
     piece = pltpu.VMEM((4, 4, 64, 256), jnp.bfloat16)
     rows = pltpu.VMEM((4, 8, CAP), jnp.int32)
@@ -326,7 +338,7 @@
         out_shape=(
             pltpu.VMEM((4, 2, 16, CAP), jnp.int32), piece, piece, pltpu.VMEM(table.shape, jnp.float32),
         ),
-        in_specs=[vmem, vmem, pl.BlockSpec(memory_space=pl.ANY)],
+        in_specs=[vmem, vmem, vmem, pl.BlockSpec(memory_space=pl.ANY)],
         out_specs=(vmem,) * 4,
         scratch_shapes=[
             rows, rows, rows, rows,
@@ -334,19 +346,9 @@
             pltpu.VMEM((NBUF, TB, 128), jnp.bfloat16),
             dma((3, 2)), dma((3, 2)), dma((13,)), dma((13,)), dma((8,)), dma((8,)), dma((NBUF,)),
         ],
-        compiler_params=pltpu.CompilerParams(collective_id=0, has_side_effects=True, vmem_limit_bytes=40 << 20),
+        compiler_params=pltpu.CompilerParams(collective_id=0, has_side_effects=True, vmem_limit_bytes=44 << 20),
         cost_estimate=pl.CostEstimate(flops=10**10, bytes_accessed=10**7, transcendentals=0),
-    )(keys, w, table)
-
-
-def make_keys(indices, pool_len):
-    n, t, p = indices.shape
-    bag = lax.broadcasted_iota(jnp.int32, (t, p, n), 2)
-    slot = lax.broadcasted_iota(jnp.int32, (t, p, n), 1)
-    idx = jnp.transpose(indices, (1, 2, 0))
-    key = ((idx >> 15) << 21) | (bag << 15) | (idx & 32767)
-    key = jnp.where(slot < pool_len[:, None, None], key, 4 << 21)
-    return jnp.transpose(key.reshape(2, 4, 4, p * n), (1, 0, 2, 3)).reshape(t, p * n)
+    )(jnp.transpose(indices, (1, 2, 0)), pool_len[None, :], w, table)
 
 
 MESH = pl.DeviceIdType.MESH
@@ -355,7 +357,7 @@
 KINDS = 18
 
 
-def dense_kernel(part, w_a, w_b, bias, scale, out, mid_a, mid_b, from_l, from_r, pooled, feats, acc, plog, lrecv, full_a, full_b, ssem, rsem, lsend, lrec, wsend, wrecv):
+def dense_kernel(part, w_a, w_b, a_left, b_left, bias, scale, out, mid_a, mid_b, from_l, from_r, pooled, feats, acc, plog, lrecv, full_a, full_b, ssem, rsem, lsend, lrec, wsend, wrecv):
     s = lax.axis_index("section")
     x = lax.axis_index("x")
     z = lax.axis_index("z")
@@ -413,43 +415,24 @@
         for kind in kinds:
             copies[c][kind].wait_recv()
 
-    right_z, left_z, far_z = lax.rem(z + 1, 4), lax.rem(z + 3, 4), lax.rem(z + 2, 4)
-
-    def w_copy(k, i, src, full, row, axis, to):
-        return pltpu.make_async_remote_copy(
-            src_ref=src.at[i] if src is not full else full.at[row, i], dst_ref=full.at[row, i],
-            send_sem=wsend.at[k, i], recv_sem=wrecv.at[k, i], device_id={axis: to}, device_id_type=MESH,
-        )
-
-    w_near, w_far = {}, {}
-    for half, (src, full, axis, mine, right, left) in enumerate(
-        ((w_a, full_a, "y", y, right_y, left_y), (w_b, full_b, "z", z, right_z, left_z))
-    ):
-        for i in range(4):
-            w_near[half, 0, i] = w_copy(half * 4, i, src, full, mine, axis, right)
-            w_near[half, 1, i] = w_copy(half * 4 + 1, i, src, full, mine, axis, left)
-        for i in range(2):
-            w_far[half, 0, i] = w_copy(half * 4 + 2, i, full, full, left, axis, right)
-            w_far[half, 1, i] = w_copy(half * 4 + 3, i + 2, full, full, right, axis, left)
-
-    def w_start(half, *pieces):
+    right_z, left_z = lax.rem(z + 1, 4), lax.rem(z + 3, 4)
+
+    def w_copies(k, src, full, row, axis, to):
+        return [
+            pltpu.make_async_remote_copy(
+                src_ref=src.at[i], dst_ref=full.at[row, i], send_sem=wsend.at[k, i], recv_sem=wrecv.at[k, i],
+                device_id={axis: to}, device_id_type=MESH,
+            )
+            for i in range(4)
+        ]
+
+    w_y = [w_copies(0, w_a, full_a, y, "y", left_y), w_copies(1, a_left, full_a, left_y, "y", right_y)]
+    w_z = [w_copies(2, w_b, full_b, z, "z", left_z), w_copies(3, b_left, full_b, left_z, "z", right_z)]
+
+    def w_start(both, *pieces):
         for i in pieces:
-            w_near[half, 0, i].start()
-            w_near[half, 1, i].start()
-
-    def w_onward(half, i):
-        w_near[half, 0, i].wait_recv()
-        w_far[half, 0, i].start()
-        w_near[half, 1, i + 2].wait_recv()
-        w_far[half, 1, i].start()
-
-    def w_arrive():
-        for half in range(2):
-            for i in range(2):
-                w_near[half, 0, i + 2].wait_recv()
-                w_near[half, 1, i].wait_recv()
-                w_far[half, 0, i].wait_recv()
-                w_far[half, 1, i].wait_recv()
+            both[0][i].start()
+            both[1][i].start()
 
     def stage_far(c):
         start(c, FAR_A, FAR_B)
@@ -487,6 +470,10 @@
         start(c, FAR_SA)
         arrive(c, FWD_B)
         start(c, FAR_SB)
+
+    columns = pl.ds(pl.multiple_of(x * 512, 512), 512)
+    bias_row = bias[:, columns].astype(jnp.float32)
+    scale_row = scale[:, columns].astype(jnp.float32)
 
     def dense_rows(first, last):
         rows = (last - first) * 128
@@ -507,34 +494,32 @@
             acc[0:rows, 256:512] += jnp.dot(lhs, rhs_b, preferred_element_type=jnp.float32)
 
         for k in range(rows // 128):
-            h = jnp.maximum(acc[k * 128:(k + 1) * 128] + bias[...], 0.0) * scale[...]
+            h = jnp.maximum(acc[k * 128:(k + 1) * 128] + bias_row, 0.0) * scale_row
             h = h[:, 0:128] + h[:, 128:256] + h[:, 256:384] + h[:, 384:512]
             plog[first + k] = jnp.sum(h.T, axis=0, keepdims=True)
 
     stage_far(0)
     stage_far(1)
-    w_start(1, 0, 2)
+    w_start(w_z, 0, 1)
     full_a[y] = w_a[...]
+    full_a[left_y] = a_left[...]
     full_b[z] = w_b[...]
+    full_b[left_z] = b_left[...]
     stages = (stage_sum, stage_pool, stage_x, stage_fwd, stage_far_s)
     for step in range(C + len(stages) - 1):
         if step == C + 3:
-            w_arrive()
+            for copy in sum(w_y + w_z, []):
+                copy.wait_recv()
             dense_rows(0, 3)
         for i, stage in enumerate(stages):
             if 0 <= step - i < C:
                 stage(step - i)
         if step == 1:
-            w_start(1, 1, 3)
+            w_start(w_z, 2)
         elif step == 2:
-            w_onward(1, 0)
+            w_start(w_z, 3)
         elif step == 3:
-            w_onward(1, 1)
-            w_start(0, 0, 2, 1, 3)
-        elif step == 5:
-            w_onward(0, 0)
-        elif step == 6:
-            w_onward(0, 1)
+            w_start(w_y, 0, 1, 2, 3)
     dense_rows(3, 4)
 
     sent = []
@@ -558,20 +543,20 @@
     for i in range(1, 8):
         total = total + lrecv[i]
     out[...] = total
-    for copy in sent + list(w_near.values()) + list(w_far.values()):
+    for copy in sent + sum(w_y + w_z, []):
         copy.wait_send()
     for c in range(C):
         for kind in range(KINDS):
             copies[c][kind].wait_send()
 
 
-def dense(partial, w_a, w_b, bias, scale):
+def dense(partial, weights, bias, scale):
     bf = jnp.bfloat16
     vmem = pl.BlockSpec(memory_space=pltpu.VMEM)
     return pl.pallas_call(
         dense_kernel,
         out_shape=jax.ShapeDtypeStruct((1, 128), jnp.float32),
-        in_specs=[vmem] * 5,
+        in_specs=[vmem] * 7,
         out_specs=vmem,
         scratch_shapes=[
             pltpu.VMEM((C, 2, 128, 128), bf),
@@ -589,25 +574,23 @@
             pltpu.SemaphoreType.DMA((KINDS, C)),
             pltpu.SemaphoreType.DMA((8,)),
             pltpu.SemaphoreType.DMA((8,)),
-            pltpu.SemaphoreType.DMA((8, 4)),
-            pltpu.SemaphoreType.DMA((8, 4)),
+            pltpu.SemaphoreType.DMA((4, 4)),
+            pltpu.SemaphoreType.DMA((4, 4)),
         ],
-        compiler_params=pltpu.CompilerParams(collective_id=1, has_side_effects=True, vmem_limit_bytes=48 << 20),
+        compiler_params=pltpu.CompilerParams(collective_id=1, has_side_effects=True, vmem_limit_bytes=20 << 20),
         cost_estimate=pl.CostEstimate(flops=3 * 10**10, bytes_accessed=10**7, transcendentals=0),
-    )(partial.reshape(4, 4, 4, 128, 128), w_a, w_b, bias, scale)
+    )(partial.reshape(4, 4, 4, 128, 128), *weights, bias, scale)
 
 
 ALL = ("section", "x", "z", "y")
 
 
 def body(indices, pool_len, tables, w_first, b_first, w_out):
-    x = lax.axis_index("x")
-    quarter = w_first.shape[1] // 4
-    bias = lax.dynamic_slice(b_first, (x * quarter,), (quarter,)).astype(jnp.float32)
-    scale = lax.dynamic_slice(w_out, (x * quarter,), (quarter,)).astype(jnp.float32)
-    lists, w_a, w_b, tab = front(make_keys(indices, pool_len), w_first, tables)
+    lists, w_a, w_b, tab = front(indices, pool_len, w_first, tables)
+    up = [(i, (i + 1) % 4) for i in range(4)]
+    weights = [w_a, w_b, lax.ppermute(w_a, "y", up), lax.ppermute(w_b, "z", up)]
     partial = lookup(lists.reshape(SRC, CAP), tab)
-    return dense(partial, w_a, w_b, bias[None, :], scale[None, :]).reshape(128)
+    return dense(partial, weights, b_first[None, :], w_out[None, :]).reshape(128)
 
 
 def solution(mesh):

time: 100 us -> 95.5 us (0.955)
  Pallas kernels: 97.5 us -> 93.6 us
  other arithmetic: 1.78 us -> 0 us
  starting transfers between devices: 0 us -> 1.41 us
    pallas_call x1, Pallas kernels: 55.1 us -> 50.8 us  [dense(): pl.pallas_call(dense_kernel, out_shape=jax.ShapeDtypeStruct((1, 128), jnp...]
    ppermute x0 -> x2, starting transfers between devices: none -> 1.41 us  [body(): weights = [w_a, w_b, lax.ppermute(w_a, 'y', up), lax.ppermute(w_b, 'z', up)]]
    select_n x1 -> x0, other arithmetic: 1 us -> none  [make_keys(): key = jnp.where(slot < pool_len[:, None, None], key, 4 << 21)]
  transfers between devices with their start and end apart: 0 -> 2, of which waited for: 0 -> 0; matrix products, arithmetic and copies ran while one was open for 0% -> 0% of each run, Pallas kernels for 0% -> 19%
where the time goes in v4:
time: 95.5 us; the launch traced here: 95.7 us
  Pallas kernels  93.6 us (98%)
  starting transfers between devices  1.41 us (1%)
    pallas_call x1, Pallas kernels, dense(): pl.pallas_call(dense_kernel, out_shape=jax.ShapeDtypeStruct((1, 128), jnp...  50.8 us
    pallas_call x1, Pallas kernels, front(): pl.pallas_call(front_kernel, out_shape=(pltpu.VMEM((4, 2, 16, CAP), jnp.i...  24.3 us
    pallas_call x1, Pallas kernels, lookup(): pl.pallas_call(lookup_kernel, out_shape=pltpu.VMEM((SRC, BAGS, 128), jnp....  18.6 us
  transfers between devices with their start and end apart: 2, of which 0 were waited for; matrix products, arithmetic and copies ran while one was open for 0% of the time, Pallas kernels for 19%

profile of v4, /device:TPU:1, one launch (start us, length us, event | category | flops | bytes accessed | tf_op | source)
XLA Modules:
  0.0 95.7 jit_solution(6435454407194610925)
XLA Ops:
  0.0 0.0 copy-start
  0.0 0.0 copy-start.1
  0.0 24.3 %shard_map.64 = (s32[4,2,16,512]{3,2,1,0:T(8,128)S(1)}, bf16[4,4,64,256]{3,2,1,0:T(8,128)(2,1)S(1)}, bf16[4,4,64,256]{3,2,1,0:T(8,128)(2,1)S(1)}, f32[32768,128]{1,0:T(8,128)S(1)}) custom-call(s32[32,8,64]{2,1,0:T(8,128)} %bitcast.8, s32[1,32]{1,0:T(1,128)} %bitcast.9, bf16[64,2048]{1,0:T(8,128)(2,1)} %w.1, bf16[32768,128]{1,0:T(8,128)(2,1)} %table.1), custom_call_target="tpu_custom_call" | custom-call | flops 10000000000 | bytes 10000000 | tf_op jit(solution)/shard_map/pallas_call | solution.py:336
  24.3 0.1 collective-permute-start
  24.4 1.3 %collective-permute-start.1 = (bf16[4,4,64,256]{3,2,1,0:T(8,128)(2,1)S(1)}, bf16[4,4,64,256]{3,2,1,0:T(8,128)(2,1)S(1)}, u32[]{:S(2)}, u32[]{:S(2)}) collective-permute-start(bf16[4,4,64,256]{3,2,1,0:T(8,128)(2,1)S(1)} %get-tuple-element.12.w_b), channel_id=1, source_target_pairs={{0,4},{4,8},{8,12},{12,0},{1,5},{5,9},{9,13},{13,1},{2,6},{6,10},{... | collective-permute-start | bytes 1572872 | tf_op jit(solution)/shard_map/ppermute | solution.py:591
  25.8 0.0 copy-done
  25.8 0.0 copy-done.1
  25.8 18.6 %shard_map.65 = bf16[128,64,128]{2,1,0:T(8,128)(2,1)S(1)} custom-call(s32[128,512]{1,0:T(8,128)S(1)} %bitcast.6, f32[32768,128]{1,0:T(8,128)S(1)} %get-tuple-element.10.tab), custom_call_target="tpu_custom_call" | custom-call | flops 10000000000 | bytes 10000000 | tf_op jit(solution)/shard_map/pallas_call | solution.py:111
  44.4 0.0 collective-permute-done.a_left
  44.4 0.0 collective-permute-done.1.b_left
  44.4 50.8 %shard_map.66 = f32[1,128]{1,0:T(1,128)S(1)} custom-call(bf16[4,4,4,128,128]{4,3,2,1,0:T(8,128)(2,1)S(1)} %bitcast.5, bf16[4,4,64,256]{3,2,1,0:T(8,128)(2,1)S(1)} %get-tuple-element.11.w_a, bf16[4,4,64,256]{3,2,1,0:T(8,128)(2,1)S(1)} %get-tuple-element.12.w_b, bf16[4,4,64,256]{3,2,1,0:T(8,128)(2,1)S(1)} %collective-permute-done.a_left, ...), custom_call_target="tpu_custom_call" | custom-call | flops 30000001024 | bytes 10000000 | tf_op jit(solution)/shard_map/pallas_call | solution.py:556
  95.1 0.5 copy.8
  (2 shorter events, 0.0 us)
Async XLA Ops:
  0.0 25.8 %copy-start = (bf16[2048]{0:T(1024)(128)(2,1)S(1)}, bf16[2048]{0:T(1024)(128)(2,1)}, u32[]{:S(2)}) copy-start(bf16[2048]{0:T(1024)(128)(2,1)} %param.10) | copy-start | bytes 12292
  0.0 25.8 %copy-start.1 = (bf16[2048]{0:T(1024)(128)(2,1)S(1)}, bf16[2048]{0:T(1024)(128)(2,1)}, u32[]{:S(2)}) copy-start(bf16[2048]{0:T(1024)(128)(2,1)} %param.11) | copy-start | bytes 12292
  24.3 20.0 %collective-permute-start = (bf16[4,4,64,256]{3,2,1,0:T(8,128)(2,1)S(1)}, bf16[4,4,64,256]{3,2,1,0:T(8,128)(2,1)S(1)}, u32[]{:S(2)}, u32[]{:S(2)}) collective-permute-start(bf16[4,4,64,256]{3,2,1,0:T(8,128)(2,1)S(1)} %get-tuple-element.11.w_a), channel_id=1, source_target_pairs={{0,1},{1,2},{2,3},{3,0},{4,5},{5,6},{6,7},{7,4},{8,9},{9,10},{10,1... | collective-permute-start | bytes 1572872 | tf_op jit(solution)/shard_map/ppermute | solution.py:591
  24.4 20.0 %collective-permute-start.1 = (bf16[4,4,64,256]{3,2,1,0:T(8,128)(2,1)S(1)}, bf16[4,4,64,256]{3,2,1,0:T(8,128)(2,1)S(1)}, u32[]{:S(2)}, u32[]{:S(2)}) collective-permute-start(bf16[4,4,64,256]{3,2,1,0:T(8,128)(2,1)S(1)} %get-tuple-element.12.w_b), channel_id=1, source_target_pairs={{0,4},{4,8},{8,12},{12,0},{1,5},{5,9},{9,13},{13,1},{2,6},{6,10},{... | collective-permute-start | bytes 1572872 | tf_op jit(solution)/shard_map/ppermute | solution.py:591

commit v5 on v4

--- a/solution.py
+++ b/solution.py
@@ -74,6 +74,14 @@
                 total = part(grp, slot, g, 0) + part(grp, slot, g, 256)
                 out[place(grp, g)] = total.astype(jnp.bfloat16)
 
+    def tail(count, slot, g, at, sizes):
+        @pl.when(count > at)
+        def _():
+            for u in range(at, at + sizes[0]):
+                buf[slot, g, u:u + 1, :] = tab[pl.ds(rows_s[slot, 1, g, u - 128], 1), :]
+            if len(sizes) > 1:
+                tail(count, slot, g, at + sizes[0], sizes[1:])
+
     @pl.loop(0, SRC // G // 2)
     def _(h):
         for slot in range(2):
@@ -92,14 +100,7 @@
                     buf[slot, g, u:u + 1, :] = tab[pl.ds(rows_s[slot, 0, g, u], 1), :]
             pool(before, 1 - slot)
             for g in range(G):
-                count = n_s[0, grp * G + g]
-                at = 0
-                for size in TAIL:
-                    @pl.when(count > 128 + at)
-                    def _(at=at, size=size):
-                        for u in range(at, at + size):
-                            buf[slot, g, 128 + u:129 + u, :] = tab[pl.ds(rows_s[slot, 1, g, u], 1), :]
-                    at += size
+                tail(n_s[0, grp * G + g], slot, g, 128, TAIL)
             long_lists(before, 1 - slot)
 
     pool(SRC // G - 1, 1)
@@ -475,16 +476,13 @@
     bias_row = bias[:, columns].astype(jnp.float32)
     scale_row = scale[:, columns].astype(jnp.float32)
 
-    def dense_rows(first, last):
+    def multiply(first, last, si):
         rows = (last - first) * 128
-        for c in range(first, last):
-            arrive(c, OWN_S, LEFT_S, RIGHT_S, FAR_SA, FAR_SB)
-        acc[0:rows] = jnp.zeros((rows, 512), jnp.float32)
-
-        @pl.loop(0, 8)
-        def _(i):
-            si, xi = i // 4, lax.rem(i, 4)
-            zi, wx = 2 * lax.rem(i, 2), i // 2
+
+        @pl.loop(0, 4)
+        def _(xi):
+            i = si * 4 + xi
+            zi, wx = 2 * lax.rem(xi, 2), i // 2
             lhs = jnp.concatenate(
                 [jnp.concatenate([feats[si, xi, c, j] for j in range(4)], axis=1) for c in range(first, last)], axis=0
             )
@@ -492,6 +490,14 @@
             acc[0:rows, 0:256] += jnp.dot(lhs, rhs_a, preferred_element_type=jnp.float32)
             rhs_b = jnp.concatenate([full_b[zi + zz, yy, wx] for zz in range(2) for yy in range(4)], axis=0)
             acc[0:rows, 256:512] += jnp.dot(lhs, rhs_b, preferred_element_type=jnp.float32)
+
+    def dense_rows(first, last):
+        rows = (last - first) * 128
+        acc[0:rows] = jnp.zeros((rows, 512), jnp.float32)
+        multiply(first, last, s)
+        for c in range(first, last):
+            arrive(c, OWN_S, LEFT_S, RIGHT_S, FAR_SA, FAR_SB)
+        multiply(first, last, other)
 
         for k in range(rows // 128):
             h = jnp.maximum(acc[k * 128:(k + 1) * 128] + bias_row, 0.0) * scale_row

time: 95.5 us -> 90.2 us (0.945)
  Pallas kernels: 93.6 us -> 88 us
    pallas_call x1, Pallas kernels: 18.6 us -> 15.1 us  [lookup(): pl.pallas_call(lookup_kernel, out_shape=pltpu.VMEM((SRC, BAGS, 128), jnp....]
    pallas_call x1, Pallas kernels: 50.8 us -> 48.5 us  [dense(): pl.pallas_call(dense_kernel, out_shape=jax.ShapeDtypeStruct((1, 128), jnp...]
  transfers between devices with their start and end apart: 2 -> 2, of which waited for: 0 -> 0; matrix products, arithmetic and copies ran while one was open for 0% -> 0% of each run, Pallas kernels for 19% -> 17%
where the time goes in v5:
time: 90.2 us; the launch traced here: 90 us
  Pallas kernels  88 us (98%)
  starting transfers between devices  1.41 us (2%)
    pallas_call x1, Pallas kernels, dense(): pl.pallas_call(dense_kernel, out_shape=jax.ShapeDtypeStruct((1, 128), jnp...  48.5 us
    pallas_call x1, Pallas kernels, front(): pl.pallas_call(front_kernel, out_shape=(pltpu.VMEM((4, 2, 16, CAP), jnp.i...  24.3 us
    pallas_call x1, Pallas kernels, lookup(): pl.pallas_call(lookup_kernel, out_shape=pltpu.VMEM((SRC, BAGS, 128), jnp....  15.1 us
  transfers between devices with their start and end apart: 2, of which 0 were waited for; matrix products, arithmetic and copies ran while one was open for 0% of the time, Pallas kernels for 17%

profile of v5, /device:TPU:1, one launch (start us, length us, event | category | flops | bytes accessed | tf_op | source)
XLA Modules:
  0.0 90.0 jit_solution(11243099950201355688)
XLA Ops:
  0.0 0.0 copy-start
  0.0 0.0 copy-start.1
  0.0 24.3 %shard_map.64 = (s32[4,2,16,512]{3,2,1,0:T(8,128)S(1)}, bf16[4,4,64,256]{3,2,1,0:T(8,128)(2,1)S(1)}, bf16[4,4,64,256]{3,2,1,0:T(8,128)(2,1)S(1)}, f32[32768,128]{1,0:T(8,128)S(1)}) custom-call(s32[32,8,64]{2,1,0:T(8,128)} %bitcast.8, s32[1,32]{1,0:T(1,128)} %bitcast.9, bf16[64,2048]{1,0:T(8,128)(2,1)} %w.1, bf16[32768,128]{1,0:T(8,128)(2,1)} %table.1), custom_call_target="tpu_custom_call" | custom-call | flops 10000000000 | bytes 10000000 | tf_op jit(solution)/shard_map/pallas_call | solution.py:337
  24.3 0.1 collective-permute-start
  24.4 1.3 %collective-permute-start.1 = (bf16[4,4,64,256]{3,2,1,0:T(8,128)(2,1)S(1)}, bf16[4,4,64,256]{3,2,1,0:T(8,128)(2,1)S(1)}, u32[]{:S(2)}, u32[]{:S(2)}) collective-permute-start(bf16[4,4,64,256]{3,2,1,0:T(8,128)(2,1)S(1)} %get-tuple-element.12.w_b), channel_id=1, source_target_pairs={{0,4},{4,8},{8,12},{12,0},{1,5},{5,9},{9,13},{13,1},{2,6},{6,10},{... | collective-permute-start | bytes 1572872 | tf_op jit(solution)/shard_map/ppermute | solution.py:597
  25.8 0.0 copy-done
  25.8 0.0 copy-done.1
  25.8 15.1 %shard_map.65 = bf16[128,64,128]{2,1,0:T(8,128)(2,1)S(1)} custom-call(s32[128,512]{1,0:T(8,128)S(1)} %bitcast.6, f32[32768,128]{1,0:T(8,128)S(1)} %get-tuple-element.10.tab), custom_call_target="tpu_custom_call" | custom-call | flops 10000000000 | bytes 10000000 | tf_op jit(solution)/shard_map/pallas_call | solution.py:112
  40.9 0.0 collective-permute-done.a_left
  40.9 0.0 collective-permute-done.1.b_left
  41.0 48.5 %shard_map.66 = f32[1,128]{1,0:T(1,128)S(1)} custom-call(bf16[4,4,4,128,128]{4,3,2,1,0:T(8,128)(2,1)S(1)} %bitcast.5, bf16[4,4,64,256]{3,2,1,0:T(8,128)(2,1)S(1)} %get-tuple-element.11.w_a, bf16[4,4,64,256]{3,2,1,0:T(8,128)(2,1)S(1)} %get-tuple-element.12.w_b, bf16[4,4,64,256]{3,2,1,0:T(8,128)(2,1)S(1)} %collective-permute-done.a_left, ...), custom_call_target="tpu_custom_call" | custom-call | flops 30000001024 | bytes 10000000 | tf_op jit(solution)/shard_map/pallas_call | solution.py:562
  89.5 0.5 copy.8
  (2 shorter events, 0.0 us)
Async XLA Ops:
  0.0 25.8 %copy-start = (bf16[2048]{0:T(1024)(128)(2,1)S(1)}, bf16[2048]{0:T(1024)(128)(2,1)}, u32[]{:S(2)}) copy-start(bf16[2048]{0:T(1024)(128)(2,1)} %param.10) | copy-start | bytes 12292
  0.0 25.8 %copy-start.1 = (bf16[2048]{0:T(1024)(128)(2,1)S(1)}, bf16[2048]{0:T(1024)(128)(2,1)}, u32[]{:S(2)}) copy-start(bf16[2048]{0:T(1024)(128)(2,1)} %param.11) | copy-start | bytes 12292
  24.3 16.6 %collective-permute-start = (bf16[4,4,64,256]{3,2,1,0:T(8,128)(2,1)S(1)}, bf16[4,4,64,256]{3,2,1,0:T(8,128)(2,1)S(1)}, u32[]{:S(2)}, u32[]{:S(2)}) collective-permute-start(bf16[4,4,64,256]{3,2,1,0:T(8,128)(2,1)S(1)} %get-tuple-element.11.w_a), channel_id=1, source_target_pairs={{0,1},{1,2},{2,3},{3,0},{4,5},{5,6},{6,7},{7,4},{8,9},{9,10},{10,1... | collective-permute-start | bytes 1572872 | tf_op jit(solution)/shard_map/ppermute | solution.py:597
  24.4 16.5 %collective-permute-start.1 = (bf16[4,4,64,256]{3,2,1,0:T(8,128)(2,1)S(1)}, bf16[4,4,64,256]{3,2,1,0:T(8,128)(2,1)S(1)}, u32[]{:S(2)}, u32[]{:S(2)}) collective-permute-start(bf16[4,4,64,256]{3,2,1,0:T(8,128)(2,1)S(1)} %get-tuple-element.12.w_b), channel_id=1, source_target_pairs={{0,4},{4,8},{8,12},{12,0},{1,5},{5,9},{9,13},{13,1},{2,6},{6,10},{... | collective-permute-start | bytes 1572872 | tf_op jit(solution)/shard_map/ppermute | solution.py:597
